TPU v7x, 32 devices: a whole 2x2x4 slice. The times are simulated.
32 devices in a mesh: section: 4 (over x, core), obs: 8 (over z, y).
Axes of the slice: x: 2, y: 2, z: 4, core: 2. Of those that a mesh axis runs over, the one named last changes fastest.
Arguments:
- predictors: bfloat16 [4, 4, 20, 32768], P('section', None, None, 'obs'), may hold values from -5 to 5
- departures: float32 [4, 4, 32768], P('section', None, 'obs'), may hold values from -30 to 30
- obs_precision: float32 [4, 4, 32768], P('section', None, 'obs'), may hold values from 0.3 to 3
- qc_pass: int32 [4, 4, 32768], P('section', None, 'obs'), may hold values 0 or 1
- block_channel: int32 [4, 4, 256], P('section', None, 'obs'), may hold values from 0 to 2047, as said below
- stream_order: int32 [4], replicated, may hold values from 0 to 3, each once
- prior_coeffs: float32 [4, 20, 2048], P(None, None, 'obs'), may hold values from -1 to 1
- prior_info: float32 [4, 210, 2048], P(None, None, 'obs'), may hold values from -1 to 32, as said below
- memory_factor: float32 [2048], P('obs'), may hold values from 0.5 to 0.98
Outputs:
- coeffs: float32 [4, 4, 20, 2048], P('section', None, None, 'obs')
- information: float32 [4, 4, 210, 2048], P('section', None, None, 'obs')
Inputs may be any that keep to these rules, and one draw needn't show every extreme that they name: `block_channel`: among the 32 row blocks of one index of obs, at most 8 have channels in any one range of the 256 channels from a multiple of 256; in every window and stream one such range holds exactly 8 blocks of every index of obs. `stream_order`: each stream appears once. `prior_info`: for every stream and channel the 210 entries are the upper triangle, row by row, of a symmetric positive definite matrix of order 20.
All inputs are finite; a program needn't handle non-finite values. No bound on the sum of `qc_pass` on one device may be relied on, other than what follows from the above.
Results may differ from a plain program's by a relative error of at most 0.0038.
Values sent between devices are 32-bit elements; how exact they have to be, the bound alone decides.
A program may use at most 64 MiB of HBM per device.

v0:
```python
import functools

import jax
import jax.numpy as jnp
import numpy as np
from jax import lax
from jax.experimental import pallas as pl
from jax.experimental.pallas import tpu as pltpu
from jax.sharding import PartitionSpec as P

HUBER_SQ = 9.0
PRIOR_WEIGHT = 64.0
F32 = jnp.float32
BF16 = jnp.bfloat16
NN = (((1,), (0,)), ((), ()))
NT = (((1,), (1,)), ((), ()))
TN = (((0,), (0,)), ((), ()))


def round_up(n, m):
    return -(-n // m) * m


def split3(x):
    hi = x.astype(BF16)
    rest = x - hi.astype(F32)
    mid = rest.astype(BF16)
    low = (rest - mid.astype(F32)).astype(BF16)
    return hi, mid, low


def dot(a, b, dims):
    return lax.dot_general(a, b, dims, preferred_element_type=F32)


def kernel(
    cfg,
    order_ref,
    x_ref,
    dep_ref,
    prec_ref,
    qc_ref,
    bc_ref,
    pc_ref,
    pi_ref,
    mf_ref,
    expand_ref,
    pick_ref,
    prefix_ref,
    co_out,
    io_out,
    co_ref,
    io_ref,
    xs,
    bcs,
    bcr,
    cs,
    cr,
    ts,
    tr,
    beta,
    state,
    work,
    info_out,
    beta_out,
    bc_send,
    bc_recv,
    c_send,
    c_recv,
    t_send,
    t_recv,
    o_send,
    o_recv,
):
    S, O, K, N, NP, T, C, NB, SL, TL = cfg
    sec = lax.axis_index("section")
    ob = lax.axis_index("obs")
    owner = sec < K
    mine = jnp.minimum(sec, K - 1)

    def send(src, dst, send_sem, recv_sem, s, o):
        here = (s == sec) & (o == ob)

        @pl.when(jnp.logical_not(here))
        def _():
            pltpu.make_async_remote_copy(
                src_ref=src,
                dst_ref=dst,
                send_sem=send_sem,
                recv_sem=recv_sem,
                device_id={"section": s, "obs": o},
                device_id_type=pl.DeviceIdType.MESH,
            ).start()

        @pl.when(here)
        def _():
            pltpu.make_async_copy(src, dst, recv_sem).start()

    def sent(src, send_sem, s, o):
        @pl.when(jnp.logical_not((s == sec) & (o == ob)))
        def _():
            pltpu.make_async_copy(src, src, send_sem).wait()

    def got(dst, recv_sem):
        pltpu.make_async_copy(dst, dst, recv_sem).wait()

    def choose(m, load):
        value = load(0)
        for i in range(1, K):
            value = jnp.where(m == i, load(i), value)
        return value

    barrier = pltpu.get_barrier_semaphore()

    def greet(s, _):
        def one(o, _):
            @pl.when(jnp.logical_not((s == sec) & (o == ob)))
            def _():
                pl.semaphore_signal(
                    barrier,
                    inc=1,
                    device_id={"section": s, "obs": o},
                    device_id_type=pl.DeviceIdType.MESH,
                )

            return 0

        return lax.fori_loop(0, O, one, 0, unroll=8 if O % 8 == 0 else 1)

    lax.fori_loop(0, S, greet, 0)
    for k in range(K):
        line = choose(order_ref[k], lambda i: bc_ref[i : i + 1, :])
        if NB < 128:
            line = jnp.concatenate([line, jnp.full((1, 128 - NB), -1, jnp.int32)], axis=1)
        bcs[k] = jnp.broadcast_to(line, (SL, 128))
    for b in range(NB):
        for i in range(N):
            xs[b, i * K : (i + 1) * K, :] = x_ref[i, :, b * 128 : (b + 1) * 128].astype(F32)
        xs[b, N * K :, :] = jnp.zeros(((NP - N) * K, 128), F32)
    beta[...] = jnp.zeros_like(beta)
    beta[0:N, :] = choose(order_ref[mine], lambda i: pc_ref[:, i, :])

    pl.semaphore_wait(barrier, S * O - 1)


    def send_channels(k, _):
        def one(o, _):
            send(bcs.at[k], bcr.at[sec, ob], bc_send.at[k, o], bc_recv.at[sec, ob], k, o)
            return 0

        return lax.fori_loop(0, O, one, 0, unroll=8 if O % 8 == 0 else 1)

    lax.fori_loop(0, K, send_channels, 0)

    rows8 = lax.broadcasted_iota(jnp.int32, (O * SL, 128), 0)
    rank_of_row = (rows8 % SL + 1).astype(F32)

    def slots(channel, low):
        inside = (channel >= low) & (channel < low + C)
        rank = dot(jnp.where(inside, 1.0, 0.0).astype(BF16), prefix_ref[...], NN)
        return inside & (rank == rank_of_row)

    @pl.when(owner)
    def _():
        def arrive(w, _):
            def one(o, _):
                got(bcr.at[w, o], bc_recv.at[w, o])
                return 0

            return lax.fori_loop(0, O, one, 0, unroll=8 if O % 8 == 0 else 1)

        lax.fori_loop(0, S, arrive, 0)

    def row_entry(k, w):
        m = order_ref[k]
        placing = slots(
            jnp.broadcast_to(bcs[k][0:1], (O * SL, 128)), (rows8 // SL) * C
        )
        placing = jnp.where(placing, 1.0, 0.0).astype(BF16)

        def one(o, _):
            got(cr.at[k, o], c_recv.at[k, o])
            return 0

        lax.fori_loop(0, O, one, 0, unroll=8 if O % 8 == 0 else 1)
        parts = split3(cr[k].reshape(O * SL, 128))
        coef3 = jnp.concatenate(
            [dot(placing, part, TN)[0:NB, 0:NP] for part in parts], axis=0
        ).astype(BF16)
        sub = lax.broadcasted_iota(jnp.int32, (8, 128), 0)
        tiles = [jnp.zeros((8, 128), F32) for _ in range(NB // 8)]
        blocks = []
        for b in range(NB):
            xb = choose(m, lambda i: xs[b, pl.ds(i, NP, stride=K), :])
            xh = xb.astype(BF16)
            blocks.append(xb)
            full = dot(coef3, xh, NN)
            q = b // 8 * 8
            tile = full[q : q + 8] + full[NB + q : NB + q + 8] + full[2 * NB + q : 2 * NB + q + 8]
            tiles[b // 8] = jnp.where(sub == b % 8, tile, tiles[b // 8])
        offset = jnp.concatenate(tiles, axis=0)
        residual = choose(m, lambda i: dep_ref[pl.ds(i, NB, stride=K), :]) - offset
        precision = choose(m, lambda i: prec_ref[pl.ds(i, NB, stride=K), :])
        passed = choose(m, lambda i: qc_ref[pl.ds(i, NB, stride=K), :]).astype(F32)
        weight = passed * precision / (1.0 + precision * residual * residual / HUBER_SQ)
        total = jnp.sum(jnp.sum(weight * residual * residual, axis=0, keepdims=True), axis=1, keepdims=True)
        count = jnp.sum(jnp.sum(passed, axis=0, keepdims=True), axis=1, keepdims=True)
        pieces = [p.astype(F32) for p in split3(residual)]
        line = lax.broadcasted_iota(jnp.int32, (NP, 128), 0)
        grams = []
        for b in range(NB):
            xb = blocks[b]
            left = (weight[b : b + 1] * xb).astype(BF16)
            right = xb
            for p in range(3):
                right = jnp.where(line == N + p, pieces[p][b : b + 1], right)
            grams.append(dot(left, right.astype(BF16), NT))
        gram = jnp.concatenate(grams, axis=0)
        spread = sum(dot(part, expand_ref[...], NN) for part in split3(gram))
        packed = jnp.sum(spread.reshape(NB, NP, TL) * pick_ref[...][None], axis=1)
        out = sum(dot(placing[:, 0:NB], part, NN) for part in split3(packed))
        lane = lax.broadcasted_iota(jnp.int32, (O * SL, TL), 1)
        out = jnp.where(lane == T + N, total, jnp.where(lane == T + N + 1, count, out))
        ts[k] = out.reshape(O, SL, TL)

        def push(o, _):
            send(ts.at[k, o], tr.at[w, ob], t_send.at[k, o], t_recv.at[w, ob], k, o)
            return 0

        lax.fori_loop(0, O, push, 0, unroll=8 if O % 8 == 0 else 1)

    def owner_slots(w):
        channel = bcr[w].reshape(O * SL, 128)
        low = ob * C
        hit = slots(channel, low)
        value = jnp.sum(jnp.where(hit, (channel - low + 1).astype(F32), 0.0), axis=1, keepdims=True)
        lane = lax.broadcasted_iota(jnp.int32, (O * SL, C), 1).astype(F32)
        return jnp.where(lane == value - 1.0, 1.0, 0.0).astype(BF16)

    def send_info(w):
        send(info_out.at[w], io_ref.at[sec], o_send.at[w, 0], o_recv.at[sec, 0], w, ob)

    def solve(w):
        hot = owner_slots(w)

        @pl.when(w == 0)
        def _():
            state[...] = choose(order_ref[mine], lambda i: pi_ref[:, i, :])

        def one(o, _):
            got(tr.at[w, o], t_recv.at[w, o])
            return 0

        lax.fori_loop(0, O, one, 0, unroll=8 if O % 8 == 0 else 1)
        terms = tr[w].reshape(O * SL, TL)
        row = lax.broadcasted_iota(jnp.int32, (O * SL, TL), 0)
        sums = jnp.sum(jnp.where(row % SL == 0, terms, 0.0), axis=0, keepdims=True)
        inverse = (sums[:, T + N + 1 : T + N + 2] + PRIOR_WEIGHT) / (sums[:, T + N : T + N + 1] + PRIOR_WEIGHT)
        normal = sum(dot(part, hot, TN) for part in split3(terms)) * inverse

        post = state[...] + normal[0:T]
        work[0:T, :] = post
        work[T:TL, :] = normal[T:TL]
        info_out[w] = post
        state[...] = post * mf_ref[...]

        @pl.when(w == S - 1)
        def _():
            send_info(w)

        cols = []
        for k in range(N):
            at = k * N - k * (k - 1) // 2 - k
            cols.append(work[at : at + NP, :])
        target = work[T : T + NP, :]
        scales, forward, starts = [], [], [0] * N
        for j in range(N):
            scale = lax.rsqrt(cols[j][j - starts[j] : j - starts[j] + 1])
            scales.append(scale)
            base = j // 8 * 8
            factor = cols[j][base - starts[j] :] * scale
            cols[j] = factor
            starts[j] = base
            step = target[j : j + 1] * scale
            forward.append(step)
            target = target - jnp.concatenate([jnp.zeros((base, C), F32), factor * step], axis=0) if base else target - factor * step
            for k in range(j + 1, N):
                kb = k // 8 * 8
                cols[k] = cols[k][kb - starts[k] :] - factor[kb - base :] * factor[k - base : k - base + 1]
                starts[k] = kb
        index = lax.broadcasted_iota(jnp.int32, (NP, C), 0)
        answer = jnp.zeros((NP, C), F32)
        for i in reversed(range(N)):
            base = i // 8 * 8
            dots = jnp.sum(cols[i] * answer[base:], axis=0, keepdims=True)
            value = (forward[i] - dots) * scales[i]
            answer = jnp.where(index == i, value, answer)
        fresh = beta[0:N, :] + answer[0:N]
        beta[0:N, :] = fresh
        beta_out[w] = fresh
        send(beta_out.at[w], co_ref.at[sec], o_send.at[w, 1], o_recv.at[sec, 1], w, ob)

    def window(w, _):
        @pl.when(owner)
        def _():
            hot = owner_slots(w)
            cs[w] = sum(dot(hot, part, NT) for part in split3(beta[...])).reshape(O, SL, 128)

            def one(o, _):
                send(cs.at[w, o], cr.at[sec, ob], c_send.at[w, o], c_recv.at[sec, ob], w, o)
                return 0

            lax.fori_loop(0, O, one, 0, unroll=8 if O % 8 == 0 else 1)

        @pl.when(sec == w)
        def _():
            def entry(i, _):
                row_entry((w + 1 + i) % K, w)
                return 0

            lax.fori_loop(0, K, entry, 0)

        @pl.when(owner & (w > 0))
        def _():
            send_info(w - 1)

        @pl.when(owner)
        def _():
            solve(w)

        return 0

    lax.fori_loop(0, S, window, 0)

    for k in range(K):
        got(io_ref.at[k], o_recv.at[k, 0])
        io_out[:, k, :] = io_ref[k]
        got(co_ref.at[k], o_recv.at[k, 1])
        co_out[:, k, :] = co_ref[k]

    def drain_rows(k, _):
        def one(o, _):
            sent(bcs.at[k], bc_send.at[k, o], k, o)
            sent(ts.at[k, o], t_send.at[k, o], k, o)
            return 0

        return lax.fori_loop(0, O, one, 0, unroll=8 if O % 8 == 0 else 1)

    lax.fori_loop(0, K, drain_rows, 0)

    @pl.when(owner)
    def _():
        def drain(w, _):
            def one(o, _):
                sent(cs.at[w, o], c_send.at[w, o], w, o)
                return 0

            lax.fori_loop(0, O, one, 0, unroll=8 if O % 8 == 0 else 1)
            sent(info_out.at[w], o_send.at[w, 0], w, ob)
            sent(beta_out.at[w], o_send.at[w, 1], w, ob)
            return 0

        lax.fori_loop(0, S, drain, 0)


def local(
    predictors,
    departures,
    obs_precision,
    qc_pass,
    block_channel,
    stream_order,
    prior_coeffs,
    prior_info,
    memory_factor,
):
    S, O = lax.axis_size("section"), lax.axis_size("obs")
    K, N, C = prior_coeffs.shape
    T = prior_info.shape[1]
    NB = block_channel.shape[2]
    R = predictors.shape[3]
    width = R // NB
    assert width == 128 and K <= S and NB <= 128 and NB % 8 == 0
    NP = round_up(N + 3, 8)
    SL = round_up(max(2 * NB // O, 1), 8)
    TL = round_up(T + N + 4, 128)
    pairs = [(i, j) for i in range(N) for j in range(i, N)]
    expand = np.zeros((NP, TL), np.float32)
    pick = np.zeros((NP, TL), np.float32)
    for t, (i, j) in enumerate(pairs):
        expand[j, t] = 1.0
        pick[i, t] = 1.0
    for i in range(N):
        expand[N : N + 3, T + i] = 1.0
        pick[i, T + i] = 1.0
    prefix = (np.arange(128)[:, None] <= np.arange(128)[None, :]).astype(np.float32)
    cfg = (S, O, K, N, NP, T, C, NB, SL, TL)

    def by_block(array):
        return array[0].reshape(K, NB, width).transpose(1, 0, 2).reshape(NB * K, width)

    vm = pl.BlockSpec(memory_space=pltpu.VMEM)
    dma = pltpu.SemaphoreType.DMA
    coeffs, info = pl.pallas_call(
        functools.partial(kernel, cfg),
        out_shape=(
            jax.ShapeDtypeStruct((N, K, C), F32),
            jax.ShapeDtypeStruct((T, K, C), F32),
        ),
        in_specs=[pl.BlockSpec(memory_space=pltpu.SMEM)] + [vm] * 11,
        out_specs=(vm, vm),
        scratch_shapes=[
            pltpu.VMEM((K, N, C), F32),
            pltpu.VMEM((K, T, C), F32),
            pltpu.VMEM((NB, NP * K, 128), F32),
            pltpu.VMEM((K, SL, 128), jnp.int32),
            pltpu.VMEM((S, O, SL, 128), jnp.int32),
            pltpu.VMEM((S, O, SL, 128), F32),
            pltpu.VMEM((K, O, SL, 128), F32),
            pltpu.VMEM((K, O, SL, TL), F32),
            pltpu.VMEM((S, O, SL, TL), F32),
            pltpu.VMEM((128, C), F32),
            pltpu.VMEM((T, C), F32),
            pltpu.VMEM((TL, C), F32),
            pltpu.VMEM((S, T, C), F32),
            pltpu.VMEM((S, N, C), F32),
            dma((K, O)),
            dma((S, O)),
            dma((S, O)),
            dma((K, O)),
            dma((K, O)),
            dma((S, O)),
            dma((S, 2)),
            dma((K, 2)),
        ],
        compiler_params=pltpu.CompilerParams(
            has_side_effects=True, collective_id=0, vmem_limit_bytes=60 * 1024 * 1024
        ),
    )(
        stream_order,
        predictors[0].transpose(1, 0, 2),
        by_block(departures),
        by_block(obs_precision),
        by_block(qc_pass),
        block_channel[0],
        prior_coeffs.transpose(1, 0, 2),
        prior_info.transpose(1, 0, 2),
        memory_factor[None],
        jnp.asarray(expand, BF16),
        jnp.asarray(pick, F32),
        jnp.asarray(prefix, BF16),
    )
    return coeffs.transpose(1, 0, 2)[None], info.transpose(1, 0, 2)[None]


def solution(mesh):
    in_specs = (
        P("section", None, None, "obs"),
        P("section", None, "obs"),
        P("section", None, "obs"),
        P("section", None, "obs"),
        P("section", None, "obs"),
        P(),
        P(None, None, "obs"),
        P(None, None, "obs"),
        P("obs"),
    )
    out_specs = (P("section", None, None, "obs"), P("section", None, None, "obs"))
    return jax.shard_map(local, mesh=mesh, in_specs=in_specs, out_specs=out_specs, check_vma=False)
```

profile of v0, /device:TPU:3, one launch (start us, length us, event | category | flops | bytes accessed | tf_op | source)
XLA Modules:
  0.0 75.4 jit_solution(12083808996000699318)
XLA Ops:
  0.6 71.0 %shard_map.131 = (f32[20,4,256]{2,1,0:T(4,128)}, f32[210,4,256]{2,1,0:T(4,128)}) custom-call(s32[4]{0:T(128)} %order_ref.1, bf16[20,4,4096]{2,1,0:T(4,128)(2,1)} %bitcast.30, f32[128,128]{1,0:T(8,128)} %bitcast.33, f32[128,128]{1,0:T(8,128)} %bitcast.34, s32[128,128]{1,0:T(8,128)} %bitcast.35, s32[4,32]{1,0:T(4,128)} %bitcast.36, f32[20,4,256]{2,1,0:T(4,128)} %bitcast.31, ...), custom_call_target="tpu_custom_call" | custom-call | tf_op jit(solution)/shard_map/pallas_call | solution.py:404
  71.7 1.5 %copy.19 = f32[1,4,20,256]{3,1,2,0:T(4,128)} copy(f32[1,4,20,256]{3,1,2,0:T(4,128)} %bitcast.32) | data formatting | bytes 163840
  73.2 2.2 %copy.20 = f32[1,4,210,256]{3,1,2,0:T(4,128)} copy(f32[1,4,210,256]{3,1,2,0:T(4,128)} %bitcast.29) | data formatting | bytes 1720320
where the time goes:
time: 75.6 us; the launch traced here: 75.4 us
  Pallas kernels  71 us (94%)
  local copies, waits for them, and re-layouts  3.74 us (5%)
    pallas_call x1, Pallas kernels, local(): pl.pallas_call(functools.partial(kernel, cfg), out_shape=(jax.ShapeDtypeS...  71 us
    unnamed x2, local copies, waits for them, and re-layouts  3.74 us

commit v1 on v0

v1 whole, which is shorter than its diff:
```python
import functools

import jax
import jax.numpy as jnp
import numpy as np
from jax import lax
from jax.experimental import pallas as pl
from jax.experimental.pallas import tpu as pltpu
from jax.sharding import PartitionSpec as P

HUBER_SQ = 9.0
PRIOR_WEIGHT = 64.0
F32 = jnp.float32
BF16 = jnp.bfloat16
NN = (((1,), (0,)), ((), ()))
NT = (((1,), (1,)), ((), ()))
TN = (((0,), (0,)), ((), ()))


def round_up(n, m):
    return -(-n // m) * m


def split3(x):
    hi = x.astype(BF16)
    rest = x - hi.astype(F32)
    mid = rest.astype(BF16)
    low = (rest - mid.astype(F32)).astype(BF16)
    return hi, mid, low


def dot(a, b, dims):
    return lax.dot_general(a, b, dims, preferred_element_type=F32)


def each(low, high, body):
    n = high - low

    def step(i, _):
        body(i)
        return 0

    lax.fori_loop(low, high, step, 0, unroll=n if n <= 8 else 1)


def iota(shape, axis):
    return lax.broadcasted_iota(jnp.int32, shape, axis)


def kernel(
    cfg,
    order_hbm,
    x_hbm,
    dep_hbm,
    prec_hbm,
    qc_hbm,
    bc_hbm,
    pc_hbm,
    pi_hbm,
    mf_hbm,
    ee_hbm,
    co_out,
    io_out,
    order_s,
    x_v,
    dep_v,
    prec_v,
    qc_v,
    bc_v,
    pc_v,
    pi_v,
    mf_v,
    ee_v,
    lists,
    bcr,
    pcs,
    pcr,
    cs,
    cr,
    ts,
    tr,
    xs,
    xh,
    pt,
    chcol,
    place,
    place_t,
    coef_v,
    hots,
    state,
    betas,
    beta_in,
    work,
    cob,
    iob,
    load_sem,
    bc_send,
    bc_recv,
    p_send,
    p_recv,
    c_send,
    c_recv,
    t_send,
    t_recv,
    f_send,
    f_recv,
    b_send,
    b_recv,
    o_send,
    o_recv,
):
    S, O, K, N, NP, T, C, NB, SL, TL = cfg
    G = S // 2
    Q = O * SL
    sec = lax.axis_index("section")
    ob = lax.axis_index("obs")
    odd = lax.rem(sec, 2) == 1
    g = sec // 2

    def remote(src, dst, send_sem, recv_sem, s, o):
        pltpu.make_async_remote_copy(
            src_ref=src,
            dst_ref=dst,
            send_sem=send_sem,
            recv_sem=recv_sem,
            device_id={"section": s, "obs": o},
            device_id_type=pl.DeviceIdType.MESH,
        ).start()

    def got(ref, sem):
        pltpu.make_async_copy(ref, ref, sem).wait()

    def fan(src, dst, send_sem, recv_sem, s):
        def one(j):
            o = lax.rem(ob + j, O)
            remote(src(o), dst, send_sem, recv_sem, s, o)

        each(1, O, one)

        @pl.when(s != sec)
        def _():
            remote(src(ob), dst, send_sem, recv_sem, s, ob)

        @pl.when(s == sec)
        def _():
            pltpu.make_async_copy(src(ob), dst, recv_sem).start()

    def fanned(like, send_sem, s):
        @pl.when(s != sec)
        def _():
            got(like, send_sem)

        @pl.when(s == sec)
        def _():
            got(like.at[0 : O - 1], send_sem)

    loads = [
        (order_hbm, order_s),
        (bc_hbm, bc_v),
        (pc_hbm, pc_v),
        (x_hbm, x_v),
        (ee_hbm, ee_v),
        (dep_hbm, dep_v),
        (prec_hbm, prec_v),
        (qc_hbm, qc_v),
        (mf_hbm, mf_v),
        (pi_hbm, pi_v),
    ]
    loads = [pltpu.make_async_copy(a, b, load_sem.at[i]) for i, (a, b) in enumerate(loads)]
    for copy in loads:
        copy.start()
    order_in, bc_in, pc_in, x_in, ee_in, dep_in, prec_in, qc_in, mf_in, pi_in = loads

    barrier = pltpu.get_barrier_semaphore()

    def greet(s):
        def one(o):
            @pl.when(jnp.logical_not((s == sec) & (o == ob)))
            def _():
                pl.semaphore_signal(
                    barrier,
                    inc=1,
                    device_id={"section": s, "obs": o},
                    device_id_type=pl.DeviceIdType.MESH,
                )

        each(0, O, one)

    lax.fori_loop(0, S, lambda s, c: (greet(s), c)[1], 0)

    bc_in.wait()
    line = bc_v[...]
    if NB < 128:
        line = jnp.concatenate([line, jnp.full((K, 128 - NB), -1, jnp.int32)], axis=1)
    lists[...] = jnp.full((8, 128), -1, jnp.int32)
    lists[0:K, :] = line
    pc_in.wait()
    for m in range(K):
        pcs[m] = jnp.zeros((NP, C), F32)
        pcs[m, 0:N, :] = pc_v[:, m, :]
        betas[m] = pcs[m]
    pl.semaphore_wait(barrier, S * O - 1)

    @pl.when(sec == 1)
    def _():
        def one(m):
            fan(lambda o: pcs.at[m], pcr.at[m, ob], p_send.at[m], p_recv.at[m], 0)

        lax.fori_loop(0, K, lambda m, c: (one(m), c)[1], 0)

    def send_lists(q):
        fan(lambda o: lists, bcr.at[sec, ob], bc_send.at[q], bc_recv.at[sec], 2 * q + 1)

    lax.fori_loop(0, G, lambda q, c: (send_lists(q), c)[1], 0)

    cs[...] = jnp.zeros_like(cs)

    eye = iota((128, 128), 0) == iota((128, 128), 1)
    upto = iota((128, 128), 0) <= iota((128, 128), 1)
    for m in range(K):
        row = jnp.broadcast_to(lists[m : m + 1, :].astype(F32), (128, 128))
        col = jnp.sum(jnp.where(eye, row, 0.0), axis=1, keepdims=True)
        range_row = jnp.floor((row + 0.5) * (1.0 / C))
        range_col = jnp.floor((col + 0.5) * (1.0 / C))
        same = range_row == range_col
        rank_row = jnp.sum(jnp.where(same & upto, 1.0, 0.0), axis=0, keepdims=True)
        back = jnp.where(same & (iota((128, 128), 0) >= iota((128, 128), 1)), 1.0, 0.0)
        rank_col = jnp.sum(back, axis=1, keepdims=True)
        chcol[m] = jnp.broadcast_to(col[0:NB], (NB, 128))
        slot = iota((Q, 128), 0)
        hit = (range_row[0:1] == (slot // SL).astype(F32)) & (rank_row == (slot % SL + 1).astype(F32))
        place[m] = jnp.where(hit, 1.0, 0.0).astype(BF16)
        slot = iota((NB, Q), 1)
        hit = (range_col[0:NB] == (slot // SL).astype(F32)) & (rank_col[0:NB] == (slot % SL + 1).astype(F32))
        place_t[m] = jnp.where(hit, 1.0, 0.0).astype(BF16)

    x_in.wait()
    ee_in.wait()

    def products(b):
        lanes = pl.ds(pl.multiple_of(b * 128, 128), 128)
        for i in range(N):
            xs[b, i * K : (i + 1) * K, :] = x_v[i, :, lanes].astype(F32)
        xs[b, N * K : (N + 1) * K, :] = jnp.ones((K, 128), F32)
        xs[b, (N + 1) * K :, :] = jnp.zeros(((NP - N - 1) * K, 128), F32)
        for m in range(K):
            xb = xs[b, pl.ds(m, NP, stride=K), :].astype(BF16)
            xh[m, :, lanes] = xb
            both = dot(xb, ee_v[...], TN)
            pt[m, lanes, :] = (both[:, 0:TL] * both[:, TL:]).astype(BF16)

    lax.fori_loop(0, NB, lambda b, c: (products(b), c)[1], 0)
    dep_in.wait()
    prec_in.wait()
    qc_in.wait()

    def split_f32(x):
        return [p.astype(F32) for p in split3(x)]

    def row_entry(m):
        @pl.when(sec == 0)
        def _():
            got(pcr.at[m], p_recv.at[m])
            channel = chcol[m]
            coef = jnp.zeros((NB, NP), F32)
            lane = iota((NB, C), 1).astype(F32)
            for o in range(O):
                wide = jnp.broadcast_to(channel[:, 0:1], (NB, C)) - float(o * C)
                hot = jnp.where(lane == wide, 1.0, 0.0).astype(BF16)
                for part in split3(pcr[m, o]):
                    coef = coef + dot(hot, part, NT)
            coef_v[...] = coef

        @pl.when(sec != 0)
        def _():
            got(cr.at[m], c_recv.at[m])
            slots = cr[m].reshape(Q, 128)[:, 0:NP]
            coef_v[...] = sum(dot(place_t[m], part, NN) for part in split3(slots))

        pieces = split_f32(coef_v[...])
        sub = iota((8, 128), 0)
        tiles = []
        for q in range(NB // 8):
            stack = jnp.concatenate([p[8 * q : 8 * q + 8] for p in pieces], axis=0).astype(BF16)
            tile = jnp.zeros((8, 128), F32)
            for c in range(4):
                at = (8 * q + 2 * c) * 128
                full = dot(stack, xh[m, :, at : at + 256], NN)
                full = full[0:8] + full[8:16] + full[16:24]
                tile = jnp.where(sub == 2 * c, full[:, 0:128], tile)
                tile = jnp.where(sub == 2 * c + 1, full[:, 128:256], tile)
            tiles.append(tile)
        offset = jnp.concatenate(tiles, axis=0)
        rows = pl.ds(m, NB, stride=K)
        residual = dep_v[rows, :] - offset
        precision = prec_v[rows, :]
        passed = qc_v[rows, :].astype(F32)
        weight = passed * precision / (1.0 + precision * residual * residual / HUBER_SQ)
        pull = weight * residual
        total = jnp.sum(jnp.sum(pull * residual, axis=0, keepdims=True), axis=1, keepdims=True)
        count = jnp.sum(jnp.sum(passed, axis=0, keepdims=True), axis=1, keepdims=True)
        weight_hi = weight.astype(BF16).astype(F32)
        weight_lo = weight - weight_hi
        pull_hi = pull.astype(BF16).astype(F32)
        pull_lo = pull - pull_hi
        group = iota((32, 128), 0) % 8
        lane = iota((8, TL), 1)
        sums = []
        for q in range(NB // 8):
            stack = jnp.concatenate(
                [v[8 * q : 8 * q + 8] for v in (weight_hi, weight_lo, pull_hi, pull_lo)], axis=0
            )
            acc = jnp.zeros((32, TL), F32)
            for c in range(4):
                at = (8 * q + 2 * c) * 128
                left = jnp.concatenate(
                    [jnp.where(group == 2 * c, stack, 0.0), jnp.where(group == 2 * c + 1, stack, 0.0)], axis=1
                )
                acc = acc + dot(left.astype(BF16), pt[m, at : at + 256, :], NN)
            sums.append(jnp.where(lane < T, acc[0:8] + acc[8:16], acc[16:24] + acc[24:32]))
        packed = jnp.concatenate(sums, axis=0)
        place_m = place[m][:, 0:NB]
        out = sum(dot(place_m, part, NN) for part in split3(packed))
        lane = iota((Q, TL), 1)
        out = jnp.where(lane == T + N, total, jnp.where(lane == T + N + 1, count, out))
        ts[m] = out.reshape(O, SL, TL)
        fan(lambda o: ts.at[m, o], tr.at[sec, m, ob], t_send.at[m], t_recv.at[sec, m], sec + 1 - lax.rem(sec, 2))

    def normal_terms(w, m):
        terms = tr[w, m].reshape(Q, TL)
        row = iota((Q, TL), 0)
        sums = jnp.sum(jnp.where(row % SL == 0, terms, 0.0), axis=0, keepdims=True)
        inverse = (sums[:, T + N + 1 : T + N + 2] + PRIOR_WEIGHT) / (sums[:, T + N : T + N + 1] + PRIOR_WEIGHT)
        return sum(dot(part, hots[w, m], TN) for part in split3(terms)) * inverse

    def solve(target_at):
        H = NP // 8
        sub = iota((8, C), 0)
        cols = []
        for k in range(N):
            at = k * N - k * (k - 1) // 2 - k
            cols.append([work[at + 8 * h : at + 8 * h + 8, :] for h in range(H)])
        right = [work[target_at + 8 * h : target_at + 8 * h + 8, :] for h in range(H)]
        scale = [jnp.ones((8, C), F32) for _ in range(H)]
        for j in range(N):
            h, r = j // 8, j % 8
            col = cols[j]
            root = lax.rsqrt(jnp.broadcast_to(col[h][r : r + 1], (8, C)))
            inverse = root * root
            factor = [v * inverse for v in col]
            factor[h] = jnp.where(sub == r, 0.0, factor[h])
            scale[h] = jnp.where(sub == r, inverse, scale[h])
            step = jnp.broadcast_to(right[h][r : r + 1], (8, C))
            right = [right[i] - factor[i] * step for i in range(H)]
            for k in range(j + 1, N):
                kh, kr = k // 8, k % 8
                pivot = jnp.broadcast_to(col[kh][kr : kr + 1], (8, C))
                for i in range(H):
                    if i >= kh or i < h or (i == h and r > 0):
                        cols[k][i] = cols[k][i] - factor[i] * pivot
                cols[k][h] = jnp.where(sub == r, pivot, cols[k][h])
        return jnp.concatenate([right[i] * scale[i] for i in range(H)], axis=0)

    def hub_entry(w, par, m):
        got(tr.at[w, m], t_recv.at[w, m])
        for q in range(1, G):

            @pl.when(q > g)
            def _():
                remote(tr.at[w, m], tr.at[w, m], f_send.at[par, m, q], f_recv.at[w, m], 2 * q + 1, ob)

        @pl.when((par == 0) & (g > 0))
        def _():
            got(beta_in.at[m], b_recv.at[m])
            betas[m] = beta_in[m]

        normal = normal_terms(w, m)
        post = state[m] + normal[0:T]
        work[0:T, :] = post
        work[T:TL, :] = normal[T:TL]
        state[m] = post * mf_v[...]
        iob[par, m] = post
        fresh = betas[m] + jnp.where(iota((NP, C), 0) < N, solve(T), 0.0)
        betas[m] = fresh
        cob[par, m] = fresh

        @pl.when(w + 1 < S)
        def _():
            hot = hots[w + 1, m]
            slots = sum(dot(hot, part, NT) for part in split3(fresh))
            cs[par, m, :, :, 0:NP] = slots.reshape(O, SL, NP)
            fan(lambda o: cs.at[par, m, o], cr.at[m, ob], c_send.at[par, m], c_recv.at[m], w + 1)

        @pl.when(par == 0)
        def _():
            remote(iob.at[0, m], iob.at[1, m], o_send.at[m, 0], o_recv.at[m, 0], sec - 1, ob)
            remote(cob.at[0, m], cob.at[1, m], o_send.at[m, 1], o_recv.at[m, 1], sec - 1, ob)

        @pl.when((par == 1) & (g + 1 < G))
        def _():
            remote(cob.at[1, m], beta_in.at[m], b_send.at[m], b_recv.at[m], sec + 2, ob)

    def hub_begin():
        pi_in.wait()
        mf_in.wait()
        for m in range(K):
            state[m] = pi_v[:, m, :]
        low = ob * C
        prefix = jnp.where(iota((128, 128), 0) <= iota((128, 128), 1), 1.0, 0.0).astype(BF16)
        rank_of_row = (iota((Q, 128), 0) % SL + 1).astype(F32)
        lane = iota((Q, C), 1).astype(F32)

        def window_hots(w):
            got(bcr.at[w], bc_recv.at[w])
            for m in range(K):
                channel = jnp.concatenate(
                    [jnp.broadcast_to(bcr[w, o, m : m + 1, :], (SL, 128)) for o in range(O)], axis=0
                )
                inside = (channel >= low) & (channel < low + C)
                rank = dot(jnp.where(inside, 1.0, 0.0).astype(BF16), prefix, NN)
                hit = inside & (rank == rank_of_row)
                value = jnp.sum(jnp.where(hit, (channel - low + 1).astype(F32), 0.0), axis=1, keepdims=True)
                hots[w, m] = jnp.where(lane == value - 1.0, 1.0, 0.0).astype(BF16)

        lax.fori_loop(0, S, lambda w, c: (window_hots(w), c)[1], 0)

        def earlier(w):
            def one(m):
                got(tr.at[w, m], f_recv.at[w, m])
                state[m] = (state[m] + normal_terms(w, m)[0:T]) * mf_v[...]

            lax.fori_loop(0, K, lambda m, c: (one(m), c)[1], 0)

        lax.fori_loop(0, 2 * g, lambda w, c: (earlier(w), c)[1], 0)

    @pl.when(odd)
    def _():
        hub_begin()

    @pl.when(jnp.logical_not(odd))
    def _():
        pi_in.wait()
        mf_in.wait()

    def turn(par):
        @pl.when(odd)
        def _():
            lax.fori_loop(0, K, lambda m, c: (hub_entry(2 * g + par, par, m), c)[1], 0)

        @pl.when(par == 0)
        def _():
            lax.fori_loop(0, K, lambda m, c: (row_entry(m), c)[1], 0)

    lax.fori_loop(0, 2, lambda par, c: (turn(par), c)[1], 0)

    @pl.when(jnp.logical_not(odd))
    def _():
        for m in range(K):
            got(iob.at[1, m], o_recv.at[m, 0])
            got(cob.at[1, m], o_recv.at[m, 1])

    order_in.wait()
    for k in range(K):
        m = order_s[k]
        io_out[:, k, :] = iob[1, m]
        co_out[:, k, :] = cob[1, m, 0:N, :]

    def drain(m):
        @pl.when(sec == 1)
        def _():
            got(pcr.at[m], p_send.at[m])

        fanned(ts.at[m], t_send.at[m], sec + 1 - lax.rem(sec, 2))

        @pl.when(odd)
        def _():
            fanned(cr.at[m], c_send.at[0, m], sec)

            @pl.when(sec + 1 < S)
            def _():
                fanned(cr.at[m], c_send.at[1, m], sec + 1)
                got(betas.at[m], b_send.at[m])

            for par in range(2):
                for q in range(1, G):

                    @pl.when(q > g)
                    def _():
                        got(ts.at[m], f_send.at[par, m, q])

            got(iob.at[0, m], o_send.at[m, 0])
            got(cob.at[0, m], o_send.at[m, 1])

    lax.fori_loop(0, K, lambda m, c: (drain(m), c)[1], 0)
    for q in range(G):
        fanned(bcr.at[0], bc_send.at[q], 2 * q + 1)


def local(
    predictors,
    departures,
    obs_precision,
    qc_pass,
    block_channel,
    stream_order,
    prior_coeffs,
    prior_info,
    memory_factor,
):
    S, O = lax.axis_size("section"), lax.axis_size("obs")
    K, N, C = prior_coeffs.shape
    T = prior_info.shape[1]
    NB = block_channel.shape[2]
    R = predictors.shape[3]
    width = R // NB
    assert width == 128 and S % 2 == 0 and K <= 8 and NB <= 128 and NB % 8 == 0
    NP = round_up(N + 1, 8)
    SL = round_up(max(2 * NB // O, 1), 8)
    TL = round_up(T + NP + 2, 128)
    G, Q = S // 2, O * SL
    pairs = [(i, j) for i in range(N) for j in range(i, N)]
    expand = np.zeros((NP, 2 * TL), np.float32)
    for t, (i, j) in enumerate(pairs):
        expand[i, t] = 1.0
        expand[j, TL + t] = 1.0
    for i in range(N):
        expand[i, T + i] = 1.0
        expand[N, TL + T + i] = 1.0
    cfg = (S, O, K, N, NP, T, C, NB, SL, TL)

    def by_block(array):
        return array[0].reshape(K, NB, width).transpose(1, 0, 2).reshape(NB * K, width)

    vm = pl.BlockSpec(memory_space=pltpu.VMEM)
    hbm = pl.BlockSpec(memory_space=pltpu.HBM)
    dma = pltpu.SemaphoreType.DMA
    coeffs, info = pl.pallas_call(
        functools.partial(kernel, cfg),
        out_shape=(
            jax.ShapeDtypeStruct((N, K, C), F32),
            jax.ShapeDtypeStruct((T, K, C), F32),
        ),
        in_specs=[hbm] * 10,
        out_specs=(vm, vm),
        scratch_shapes=[
            pltpu.SMEM((K,), jnp.int32),
            pltpu.VMEM((N, K, R), BF16),
            pltpu.VMEM((NB * K, 128), F32),
            pltpu.VMEM((NB * K, 128), F32),
            pltpu.VMEM((NB * K, 128), jnp.int32),
            pltpu.VMEM((K, NB), jnp.int32),
            pltpu.VMEM((N, K, C), F32),
            pltpu.VMEM((T, K, C), F32),
            pltpu.VMEM((1, C), F32),
            pltpu.VMEM((NP, 2 * TL), BF16),
            pltpu.VMEM((8, 128), jnp.int32),
            pltpu.VMEM((S, O, 8, 128), jnp.int32),
            pltpu.VMEM((K, NP, C), F32),
            pltpu.VMEM((K, O, NP, C), F32),
            pltpu.VMEM((2, K, O, SL, 128), F32),
            pltpu.VMEM((K, O, SL, 128), F32),
            pltpu.VMEM((K, O, SL, TL), F32),
            pltpu.VMEM((S, K, O, SL, TL), F32),
            pltpu.VMEM((NB, NP * K, 128), F32),
            pltpu.VMEM((K, NP, R), BF16),
            pltpu.VMEM((K, R, TL), BF16),
            pltpu.VMEM((K, NB, 128), F32),
            pltpu.VMEM((K, Q, 128), BF16),
            pltpu.VMEM((K, NB, Q), BF16),
            pltpu.VMEM((NB, NP), F32),
            pltpu.VMEM((S, K, Q, C), BF16),
            pltpu.VMEM((K, T, C), F32),
            pltpu.VMEM((K, NP, C), F32),
            pltpu.VMEM((K, NP, C), F32),
            pltpu.VMEM((TL, C), F32),
            pltpu.VMEM((2, K, NP, C), F32),
            pltpu.VMEM((2, K, T, C), F32),
            dma((10,)),
            dma((G,)),
            dma((S,)),
            dma((K,)),
            dma((K,)),
            dma((2, K)),
            dma((K,)),
            dma((K,)),
            dma((S, K)),
            dma((2, K, G)),
            dma((S, K)),
            dma((K,)),
            dma((K,)),
            dma((K, 2)),
            dma((K, 2)),
        ],
        compiler_params=pltpu.CompilerParams(
            has_side_effects=True, collective_id=0, vmem_limit_bytes=48 * 1024 * 1024
        ),
    )(*(pltpu.with_memory_space_constraint(a, pltpu.HBM) for a in (
        stream_order,
        predictors[0].transpose(1, 0, 2),
        by_block(departures),
        by_block(obs_precision),
        by_block(qc_pass),
        block_channel[0],
        prior_coeffs.transpose(1, 0, 2),
        prior_info.transpose(1, 0, 2),
        memory_factor[None],
        jnp.asarray(expand, BF16),
    )))
    return coeffs.transpose(1, 0, 2)[None], info.transpose(1, 0, 2)[None]


def solution(mesh):
    in_specs = (
        P("section", None, None, "obs"),
        P("section", None, "obs"),
        P("section", None, "obs"),
        P("section", None, "obs"),
        P("section", None, "obs"),
        P(),
        P(None, None, "obs"),
        P(None, None, "obs"),
        P("obs"),
    )
    out_specs = (P("section", None, None, "obs"), P("section", None, None, "obs"))
    return jax.shard_map(local, mesh=mesh, in_specs=in_specs, out_specs=out_specs, check_vma=False)
```

time: 75.6 us -> 62 us (0.82)
  Pallas kernels: 71 us -> 59.7 us
  local copies, waits for them, and re-layouts: 3.74 us -> 1.54 us
    pallas_call x1, Pallas kernels: 71 us -> 59.7 us  [local(): pl.pallas_call(functools.partial(kernel, cfg), out_shape=(jax.ShapeDtypeS...]
    unnamed x2, local copies, waits for them, and re-layouts: 3.74 us -> 1.54 us
where the time goes in v1:
time: 62 us; the launch traced here: 61.9 us
  Pallas kernels  59.7 us (96%)
  local copies, waits for them, and re-layouts  1.54 us (2%)
  between operations  0.64 us (1%)
    pallas_call x1, Pallas kernels, local(): pl.pallas_call(functools.partial(kernel, cfg), out_shape=(jax.ShapeDtypeS...  59.7 us
    unnamed x2, local copies, waits for them, and re-layouts  1.54 us

profile of v1, /device:TPU:3, one launch (start us, length us, event | category | flops | bytes accessed | tf_op | source)
XLA Modules:
  0.0 61.9 jit_solution(4039053350836297991)
XLA Ops:
  0.6 59.7 %shard_map.113 = (f32[20,4,256]{2,1,0:T(4,128)S(1)}, f32[210,4,256]{2,1,0:T(4,128)S(1)}) custom-call(s32[4]{0:T(128)} %order_hbm.1, bf16[20,4,4096]{2,1,0:T(4,128)(2,1)} %bitcast.31, f32[128,128]{1,0:T(8,128)} %bitcast.33, f32[128,128]{1,0:T(8,128)} %bitcast.34, s32[128,128]{1,0:T(8,128)} %bitcast.35, s32[4,32]{1,0:T(4,128)} %bitcast.36, ...), custom_call_target="tpu_custom_call" | custom-call | tf_op jit(solution)/shard_map/pallas_call | solution.py:537
  60.3 0.6 %copy.17 = f32[1,4,20,256]{3,1,2,0:T(4,128)} copy(f32[1,4,20,256]{3,1,2,0:T(4,128)S(1)} %bitcast.29) | data formatting | bytes 163840
  60.9 0.9 %copy.18 = f32[1,4,210,256]{3,1,2,0:T(4,128)} copy(f32[1,4,210,256]{3,1,2,0:T(4,128)S(1)} %bitcast.28) | data formatting | bytes 1720320

commit v2 on v1

--- a/solution.py
+++ b/solution.py
@@ -90,6 +90,12 @@
     state,
     betas,
     beta_in,
+    beta_pass,
+    base,
+    held,
+    match,
+    first,
+    follow,
     work,
     cob,
     iob,
@@ -114,8 +120,13 @@
     Q = O * SL
     sec = lax.axis_index("section")
     ob = lax.axis_index("obs")
-    odd = lax.rem(sec, 2) == 1
+    core = lax.rem(sec, 2)
+    odd = core == 1
     g = sec // 2
+    mine = K // 2
+
+    def hub_of(m):
+        return 2 * g + 1 - lax.rem(m, 2)
 
     def remote(src, dst, send_sem, recv_sem, s, o):
         pltpu.make_async_remote_copy(
@@ -189,36 +200,63 @@
     lax.fori_loop(0, S, lambda s, c: (greet(s), c)[1], 0)
 
     bc_in.wait()
-    line = bc_v[...]
-    if NB < 128:
-        line = jnp.concatenate([line, jnp.full((K, 128 - NB), -1, jnp.int32)], axis=1)
-    lists[...] = jnp.full((8, 128), -1, jnp.int32)
-    lists[0:K, :] = line
+    line = [bc_v[m : m + 1, :] for m in range(K)]
+    if K * NB < 128:
+        line.append(jnp.full((1, 128 - K * NB), -1, jnp.int32))
+    lists[...] = jnp.concatenate(line, axis=1)
     pc_in.wait()
     for m in range(K):
         pcs[m] = jnp.zeros((NP, C), F32)
         pcs[m, 0:N, :] = pc_v[:, m, :]
         betas[m] = pcs[m]
+    def unpack():
+        x_in.wait()
+        ee_in.wait()
+        for b in range(NB):
+            for i in range(N):
+                xs[b, i * K : (i + 1) * K, :] = x_v[i, :, b * 128 : (b + 1) * 128].astype(F32)
+            xs[b, N * K : (N + 1) * K, :] = jnp.ones((K, 128), F32)
+            xs[b, (N + 1) * K :, :] = jnp.zeros(((NP - N - 1) * K, 128), F32)
+
+    def products(low, high):
+        def one(b):
+            lanes = pl.ds(pl.multiple_of(b * 128, 128), 128)
+            for m in range(low, high):
+                xb = xs[b, pl.ds(m, NP, stride=K), :].astype(BF16)
+                xh[m, :, lanes] = xb
+                both = dot(xb, ee_v[...], TN)
+                pt[m, lanes, :] = (both[:, 0:TL] * both[:, TL:]).astype(BF16)
+
+        lax.fori_loop(0, NB, lambda b, c: (one(b), c)[1], 0, unroll=4)
+
+    @pl.when(jnp.logical_not(odd))
+    def _():
+        unpack()
+        products(0, K // 2)
+
     pl.semaphore_wait(barrier, S * O - 1)
 
-    @pl.when(sec == 1)
-    def _():
-        def one(m):
+    def send_lists(s):
+        fan(lambda o: lists, bcr.at[sec, ob], bc_send.at[s], bc_recv.at[sec], s)
+
+    lax.fori_loop(0, S, lambda s, c: (send_lists(s), c)[1], 0)
+
+    def send_prior(m):
+        @pl.when(sec == 2 * lax.rem(m, G) + 1)
+        def _():
             fan(lambda o: pcs.at[m], pcr.at[m, ob], p_send.at[m], p_recv.at[m], 0)
 
-        lax.fori_loop(0, K, lambda m, c: (one(m), c)[1], 0)
-
-    def send_lists(q):
-        fan(lambda o: lists, bcr.at[sec, ob], bc_send.at[q], bc_recv.at[sec], 2 * q + 1)
-
-    lax.fori_loop(0, G, lambda q, c: (send_lists(q), c)[1], 0)
+    lax.fori_loop(0, K, lambda m, c: (send_prior(m), c)[1], 0)
 
     cs[...] = jnp.zeros_like(cs)
 
     eye = iota((128, 128), 0) == iota((128, 128), 1)
     upto = iota((128, 128), 0) <= iota((128, 128), 1)
     for m in range(K):
-        row = jnp.broadcast_to(lists[m : m + 1, :].astype(F32), (128, 128))
+        row = bc_v[m : m + 1, :].astype(F32)
+        if NB < 128:
+            row = jnp.concatenate([row, jnp.full((1, 128 - NB), -1.0, F32)], axis=1)
+        row = jnp.broadcast_to(row, (128, 128))
         col = jnp.sum(jnp.where(eye, row, 0.0), axis=1, keepdims=True)
         range_row = jnp.floor((row + 0.5) * (1.0 / C))
         range_col = jnp.floor((col + 0.5) * (1.0 / C))
@@ -234,22 +272,13 @@
         hit = (range_col[0:NB] == (slot // SL).astype(F32)) & (rank_col[0:NB] == (slot % SL + 1).astype(F32))
         place_t[m] = jnp.where(hit, 1.0, 0.0).astype(BF16)
 
-    x_in.wait()
-    ee_in.wait()
-
-    def products(b):
-        lanes = pl.ds(pl.multiple_of(b * 128, 128), 128)
-        for i in range(N):
-            xs[b, i * K : (i + 1) * K, :] = x_v[i, :, lanes].astype(F32)
-        xs[b, N * K : (N + 1) * K, :] = jnp.ones((K, 128), F32)
-        xs[b, (N + 1) * K :, :] = jnp.zeros(((NP - N - 1) * K, 128), F32)
-        for m in range(K):
-            xb = xs[b, pl.ds(m, NP, stride=K), :].astype(BF16)
-            xh[m, :, lanes] = xb
-            both = dot(xb, ee_v[...], TN)
-            pt[m, lanes, :] = (both[:, 0:TL] * both[:, TL:]).astype(BF16)
-
-    lax.fori_loop(0, NB, lambda b, c: (products(b), c)[1], 0)
+    @pl.when(odd)
+    def _():
+        unpack()
+        products(0, K // 2)
+
+    products(K // 2, K)
+
     dep_in.wait()
     prec_in.wait()
     qc_in.wait()
@@ -324,81 +353,96 @@
         lane = iota((Q, TL), 1)
         out = jnp.where(lane == T + N, total, jnp.where(lane == T + N + 1, count, out))
         ts[m] = out.reshape(O, SL, TL)
-        fan(lambda o: ts.at[m, o], tr.at[sec, m, ob], t_send.at[m], t_recv.at[sec, m], sec + 1 - lax.rem(sec, 2))
-
-    def normal_terms(w, m):
-        terms = tr[w, m].reshape(Q, TL)
+        fan(lambda o: ts.at[m, o], tr.at[sec, m, ob], t_send.at[m], t_recv.at[sec, m], hub_of(m))
+
+    def scale_of(terms):
         row = iota((Q, TL), 0)
         sums = jnp.sum(jnp.where(row % SL == 0, terms, 0.0), axis=0, keepdims=True)
-        inverse = (sums[:, T + N + 1 : T + N + 2] + PRIOR_WEIGHT) / (sums[:, T + N : T + N + 1] + PRIOR_WEIGHT)
-        return sum(dot(part, hots[w, m], TN) for part in split3(terms)) * inverse
-
-    def solve(target_at):
+        return (sums[:, T + N + 1 : T + N + 2] + PRIOR_WEIGHT) / (sums[:, T + N : T + N + 1] + PRIOR_WEIGHT)
+
+    def solve():
         H = NP // 8
-        sub = iota((8, C), 0)
+        sub = iota((8, Q), 0)
         cols = []
         for k in range(N):
             at = k * N - k * (k - 1) // 2 - k
             cols.append([work[at + 8 * h : at + 8 * h + 8, :] for h in range(H)])
-        right = [work[target_at + 8 * h : target_at + 8 * h + 8, :] for h in range(H)]
-        scale = [jnp.ones((8, C), F32) for _ in range(H)]
+        right = [work[T + 8 * h : T + 8 * h + 8, :] for h in range(H)]
+        scale = [jnp.ones((8, Q), F32) for _ in range(H)]
         for j in range(N):
             h, r = j // 8, j % 8
             col = cols[j]
-            root = lax.rsqrt(jnp.broadcast_to(col[h][r : r + 1], (8, C)))
+            root = lax.rsqrt(jnp.broadcast_to(col[h][r : r + 1], (8, Q)))
             inverse = root * root
             factor = [v * inverse for v in col]
             factor[h] = jnp.where(sub == r, 0.0, factor[h])
             scale[h] = jnp.where(sub == r, inverse, scale[h])
-            step = jnp.broadcast_to(right[h][r : r + 1], (8, C))
+            step = jnp.broadcast_to(right[h][r : r + 1], (8, Q))
             right = [right[i] - factor[i] * step for i in range(H)]
             for k in range(j + 1, N):
                 kh, kr = k // 8, k % 8
-                pivot = jnp.broadcast_to(col[kh][kr : kr + 1], (8, C))
+                pivot = jnp.broadcast_to(col[kh][kr : kr + 1], (8, Q))
                 for i in range(H):
                     if i >= kh or i < h or (i == h and r > 0):
                         cols[k][i] = cols[k][i] - factor[i] * pivot
                 cols[k][h] = jnp.where(sub == r, pivot, cols[k][h])
         return jnp.concatenate([right[i] * scale[i] for i in range(H)], axis=0)
 
-    def hub_entry(w, par, m):
+    def hub_ready(par, m):
+        w = 2 * g + par
+
+        @pl.when(w + 1 < S)
+        def _():
+            base[m] = sum(dot(hots[w + 1, m], part, NT) for part in split3(betas[m]))
+
+        held[m] = sum(dot(part, hots[w, m], NT) for part in split3(state[m]))
+
+    def hub_entry(par, m):
+        w = 2 * g + par
+        hot = hots[w, m]
         got(tr.at[w, m], t_recv.at[w, m])
         for q in range(1, G):
 
             @pl.when(q > g)
             def _():
-                remote(tr.at[w, m], tr.at[w, m], f_send.at[par, m, q], f_recv.at[w, m], 2 * q + 1, ob)
-
-        @pl.when((par == 0) & (g > 0))
-        def _():
-            got(beta_in.at[m], b_recv.at[m])
-            betas[m] = beta_in[m]
-
-        normal = normal_terms(w, m)
-        post = state[m] + normal[0:T]
-        work[0:T, :] = post
+                remote(tr.at[w, m], tr.at[w, m], f_send.at[par, m, q], f_recv.at[w, m], 2 * q + core, ob)
+
+        terms = tr[w, m].reshape(Q, TL)
+        parts = split3(terms)
+        inverse = scale_of(terms)
+        normal = sum(dot(part, match[par, m], TN) for part in parts) * inverse
+        work[0:T, :] = held[m] + normal[0:T]
         work[T:TL, :] = normal[T:TL]
-        state[m] = post * mf_v[...]
-        iob[par, m] = post
-        fresh = betas[m] + jnp.where(iota((NP, C), 0) < N, solve(T), 0.0)
-        betas[m] = fresh
-        cob[par, m] = fresh
+        filled = work[0:1, :] > 0.0
+        delta = jnp.where((iota((NP, Q), 0) < N) & filled, solve(), 0.0)
+        deltas = split3(delta)
 
         @pl.when(w + 1 < S)
         def _():
-            hot = hots[w + 1, m]
-            slots = sum(dot(hot, part, NT) for part in split3(fresh))
+            slots = base[m] + sum(dot(follow[par, m], part, NT) for part in deltas)
             cs[par, m, :, :, 0:NP] = slots.reshape(O, SL, NP)
             fan(lambda o: cs.at[par, m, o], cr.at[m, ob], c_send.at[par, m], c_recv.at[m], w + 1)
 
-        @pl.when(par == 0)
-        def _():
-            remote(iob.at[0, m], iob.at[1, m], o_send.at[m, 0], o_recv.at[m, 0], sec - 1, ob)
-            remote(cob.at[0, m], cob.at[1, m], o_send.at[m, 1], o_recv.at[m, 1], sec - 1, ob)
+        here = jnp.where(w == sec, 1, 0)
+        fresh = betas[m] + sum(dot(part, first[par, m], NN) for part in deltas)
+        betas[m] = fresh
+        cob[here, m] = fresh
+        post = state[m] + sum(dot(part, hot, TN) for part in parts)[0:T] * inverse
+        iob[here, m] = post
+        state[m] = post * mf_v[...]
+
+        @pl.when(w != sec)
+        def _():
+            remote(iob.at[0, m], iob.at[1, m], o_send.at[m, 0], o_recv.at[m, 0], w, ob)
+            remote(cob.at[0, m], cob.at[1, m], o_send.at[m, 1], o_recv.at[m, 1], w, ob)
 
         @pl.when((par == 1) & (g + 1 < G))
         def _():
-            remote(cob.at[1, m], beta_in.at[m], b_send.at[m], b_recv.at[m], sec + 2, ob)
+            beta_pass[m] = fresh
+            remote(beta_pass.at[m], beta_in.at[m], b_send.at[m], b_recv.at[m], sec + 2, ob)
+
+    def stream(i):
+        return 2 * i + 1 - core
 
     def hub_begin():
         pi_in.wait()
@@ -410,55 +454,81 @@
         rank_of_row = (iota((Q, 128), 0) % SL + 1).astype(F32)
         lane = iota((Q, C), 1).astype(F32)
 
+        for w in range(S):
+            got(bcr.at[w], bc_recv.at[w])
+        owner_lane = iota((Q, 128), 1) // NB
+
         def window_hots(w):
-            got(bcr.at[w], bc_recv.at[w])
-            for m in range(K):
-                channel = jnp.concatenate(
-                    [jnp.broadcast_to(bcr[w, o, m : m + 1, :], (SL, 128)) for o in range(O)], axis=0
-                )
-                inside = (channel >= low) & (channel < low + C)
-                rank = dot(jnp.where(inside, 1.0, 0.0).astype(BF16), prefix, NN)
-                hit = inside & (rank == rank_of_row)
+            channel = jnp.concatenate([jnp.broadcast_to(bcr[w, o], (SL, 128)) for o in range(O)], axis=0)
+            inside = (channel >= low) & (channel < low + C)
+            for i in range(mine):
+                ours = inside & (owner_lane == stream(i))
+                rank = dot(jnp.where(ours, 1.0, 0.0).astype(BF16), prefix, NN)
+                hit = ours & (rank == rank_of_row)
                 value = jnp.sum(jnp.where(hit, (channel - low + 1).astype(F32), 0.0), axis=1, keepdims=True)
-                hots[w, m] = jnp.where(lane == value - 1.0, 1.0, 0.0).astype(BF16)
-
-        lax.fori_loop(0, S, lambda w, c: (window_hots(w), c)[1], 0)
+                hots[w, stream(i)] = jnp.where(lane == value - 1.0, 1.0, 0.0).astype(BF16)
+
+        each(0, S, window_hots)
+        earlier_slot = iota((Q, Q), 1) < iota((Q, Q), 0)
+
+        def links(par, i):
+            m = stream(i)
+            w = 2 * g + par
+            hot = hots[w, m]
+            same = dot(hot, hot, NT)
+            match[par, m] = same.astype(BF16)
+            copies = jnp.sum(jnp.where(earlier_slot, same, 0.0), axis=1, keepdims=True)
+            lead = jnp.where(copies == 0.0, hot.astype(F32), 0.0).astype(BF16)
+            first[par, m] = lead
+
+            after = jnp.minimum(w + 1, S - 1)
+            follow[par, m] = dot(hots[after, m], lead, NT).astype(BF16)
+
+        for i in range(mine):
+            for par in range(2):
+                links(par, i)
 
         def earlier(w):
-            def one(m):
+            def one(i):
+                m = stream(i)
                 got(tr.at[w, m], f_recv.at[w, m])
-                state[m] = (state[m] + normal_terms(w, m)[0:T]) * mf_v[...]
-
-            lax.fori_loop(0, K, lambda m, c: (one(m), c)[1], 0)
+                terms = tr[w, m].reshape(Q, TL)
+                normal = sum(dot(part, hots[w, m], TN) for part in split3(terms))[0:T] * scale_of(terms)
+                state[m] = (state[m] + normal) * mf_v[...]
+
+            lax.fori_loop(0, mine, lambda i, c: (one(i), c)[1], 0)
 
         lax.fori_loop(0, 2 * g, lambda w, c: (earlier(w), c)[1], 0)
 
-    @pl.when(odd)
-    def _():
-        hub_begin()
-
-    @pl.when(jnp.logical_not(odd))
-    def _():
-        pi_in.wait()
-        mf_in.wait()
+        @pl.when(g > 0)
+        def _():
+            def take(i):
+                m = stream(i)
+                got(beta_in.at[m], b_recv.at[m])
+                betas[m] = beta_in[m]
+
+            lax.fori_loop(0, mine, lambda i, c: (take(i), c)[1], 0)
 
     def turn(par):
-        @pl.when(odd)
-        def _():
-            lax.fori_loop(0, K, lambda m, c: (hub_entry(2 * g + par, par, m), c)[1], 0)
+        @pl.when(par == core)
+        def _():
+            lax.fori_loop(0, K, lambda m, c: (row_entry(m), c)[1], 0)
 
         @pl.when(par == 0)
         def _():
-            lax.fori_loop(0, K, lambda m, c: (row_entry(m), c)[1], 0)
+            hub_begin()
+
+        lax.fori_loop(0, mine, lambda i, c: (hub_ready(par, stream(i)), c)[1], 0)
+        lax.fori_loop(0, mine, lambda i, c: (hub_entry(par, stream(i)), c)[1], 0)
 
     lax.fori_loop(0, 2, lambda par, c: (turn(par), c)[1], 0)
 
-    @pl.when(jnp.logical_not(odd))
-    def _():
-        for m in range(K):
-            got(iob.at[1, m], o_recv.at[m, 0])
-            got(cob.at[1, m], o_recv.at[m, 1])
-
+    def arrive(i):
+        m = 2 * i + core
+        got(iob.at[1, m], o_recv.at[m, 0])
+        got(cob.at[1, m], o_recv.at[m, 1])
+
+    lax.fori_loop(0, K - mine, lambda i, c: (arrive(i), c)[1], 0)
     order_in.wait()
     for k in range(K):
         m = order_s[k]
@@ -466,34 +536,34 @@
         co_out[:, k, :] = cob[1, m, 0:N, :]
 
     def drain(m):
-        @pl.when(sec == 1)
+        @pl.when(sec == 2 * lax.rem(m, G) + 1)
         def _():
             got(pcr.at[m], p_send.at[m])
 
-        fanned(ts.at[m], t_send.at[m], sec + 1 - lax.rem(sec, 2))
-
-        @pl.when(odd)
-        def _():
-            fanned(cr.at[m], c_send.at[0, m], sec)
-
-            @pl.when(sec + 1 < S)
-            def _():
-                fanned(cr.at[m], c_send.at[1, m], sec + 1)
-                got(betas.at[m], b_send.at[m])
-
-            for par in range(2):
-                for q in range(1, G):
-
-                    @pl.when(q > g)
-                    def _():
-                        got(ts.at[m], f_send.at[par, m, q])
-
-            got(iob.at[0, m], o_send.at[m, 0])
-            got(cob.at[0, m], o_send.at[m, 1])
-
+        fanned(ts.at[m], t_send.at[m], hub_of(m))
+
+    def drain_hub(i):
+        m = stream(i)
+        fanned(cr.at[m], c_send.at[0, m], 2 * g + 1)
+
+        @pl.when(g + 1 < G)
+        def _():
+            fanned(cr.at[m], c_send.at[1, m], 2 * g + 2)
+            got(betas.at[m], b_send.at[m])
+
+        for par in range(2):
+            for q in range(1, G):
+
+                @pl.when(q > g)
+                def _():
+                    got(ts.at[m], f_send.at[par, m, q])
+
+        got(iob.at[0, m], o_send.at[m, 0])
+        got(cob.at[0, m], o_send.at[m, 1])
+
+    lax.fori_loop(0, mine, lambda i, c: (drain_hub(i), c)[1], 0)
     lax.fori_loop(0, K, lambda m, c: (drain(m), c)[1], 0)
-    for q in range(G):
-        fanned(bcr.at[0], bc_send.at[q], 2 * q + 1)
+    lax.fori_loop(0, S, lambda s, c: (fanned(bcr.at[0], bc_send.at[s], s), c)[1], 0)
 
 
 def local(
@@ -513,7 +583,7 @@
     NB = block_channel.shape[2]
     R = predictors.shape[3]
     width = R // NB
-    assert width == 128 and S % 2 == 0 and K <= 8 and NB <= 128 and NB % 8 == 0
+    assert width == 128 and S % 2 == 0 and K % 2 == 0 and K * NB <= 128 and NB % 8 == 0
     NP = round_up(N + 1, 8)
     SL = round_up(max(2 * NB // O, 1), 8)
     TL = round_up(T + NP + 2, 128)
@@ -553,8 +623,8 @@
             pltpu.VMEM((T, K, C), F32),
             pltpu.VMEM((1, C), F32),
             pltpu.VMEM((NP, 2 * TL), BF16),
-            pltpu.VMEM((8, 128), jnp.int32),
-            pltpu.VMEM((S, O, 8, 128), jnp.int32),
+            pltpu.VMEM((1, 128), jnp.int32),
+            pltpu.VMEM((S, O, 1, 128), jnp.int32),
             pltpu.VMEM((K, NP, C), F32),
             pltpu.VMEM((K, O, NP, C), F32),
             pltpu.VMEM((2, K, O, SL, 128), F32),
@@ -572,11 +642,17 @@
             pltpu.VMEM((K, T, C), F32),
             pltpu.VMEM((K, NP, C), F32),
             pltpu.VMEM((K, NP, C), F32),
-            pltpu.VMEM((TL, C), F32),
+            pltpu.VMEM((K, NP, C), F32),
+            pltpu.VMEM((K, Q, NP), F32),
+            pltpu.VMEM((K, T, Q), F32),
+            pltpu.VMEM((2, K, Q, Q), BF16),
+            pltpu.VMEM((2, K, Q, C), BF16),
+            pltpu.VMEM((2, K, Q, Q), BF16),
+            pltpu.VMEM((TL, Q), F32),
             pltpu.VMEM((2, K, NP, C), F32),
             pltpu.VMEM((2, K, T, C), F32),
             dma((10,)),
-            dma((G,)),
+            dma((S,)),
             dma((S,)),
             dma((K,)),
             dma((K,)),

time: 62 us -> 55.5 us (0.90)
  Pallas kernels: 59.7 us -> 53.2 us
    pallas_call x1, Pallas kernels: 59.7 us -> 53.2 us  [local(): pl.pallas_call(functools.partial(kernel, cfg), out_shape=(jax.ShapeDtypeS...]
where the time goes in v2:
time: 55.5 us; the launch traced here: 55.4 us
  Pallas kernels  53.2 us (96%)
  local copies, waits for them, and re-layouts  1.54 us (3%)
  between operations  0.64 us (1%)
    pallas_call x1, Pallas kernels, local(): pl.pallas_call(functools.partial(kernel, cfg), out_shape=(jax.ShapeDtypeS...  53.2 us
    unnamed x2, local copies, waits for them, and re-layouts  1.54 us

profile of v2, /device:TPU:3, one launch (start us, length us, event | category | flops | bytes accessed | tf_op | source)
XLA Modules:
  0.0 55.4 jit_solution(12480260286549248933)
XLA Ops:
  0.6 53.2 %shard_map.113 = (f32[20,4,256]{2,1,0:T(4,128)S(1)}, f32[210,4,256]{2,1,0:T(4,128)S(1)}) custom-call(s32[4]{0:T(128)} %order_hbm.1, bf16[20,4,4096]{2,1,0:T(4,128)(2,1)} %bitcast.31, f32[128,128]{1,0:T(8,128)} %bitcast.33, f32[128,128]{1,0:T(8,128)} %bitcast.34, s32[128,128]{1,0:T(8,128)} %bitcast.35, s32[4,32]{1,0:T(4,128)} %bitcast.36, ...), custom_call_target="tpu_custom_call" | custom-call | tf_op jit(solution)/shard_map/pallas_call | solution.py:607
  53.8 0.6 %copy.17 = f32[1,4,20,256]{3,1,2,0:T(4,128)} copy(f32[1,4,20,256]{3,1,2,0:T(4,128)S(1)} %bitcast.29) | data formatting | bytes 163840
  54.5 0.9 %copy.18 = f32[1,4,210,256]{3,1,2,0:T(4,128)} copy(f32[1,4,210,256]{3,1,2,0:T(4,128)S(1)} %bitcast.28) | data formatting | bytes 1720320

commit v3 on v2

--- a/solution.py
+++ b/solution.py
@@ -90,7 +90,8 @@
     state,
     betas,
     beta_in,
-    beta_pass,
+    beta_mid,
+    state_in,
     base,
     held,
     match,
@@ -112,6 +113,9 @@
     f_recv,
     b_send,
     b_recv,
+    s_send,
+    h_send,
+    h_recv,
     o_send,
     o_recv,
 ):
@@ -123,10 +127,7 @@
     core = lax.rem(sec, 2)
     odd = core == 1
     g = sec // 2
-    mine = K // 2
-
-    def hub_of(m):
-        return 2 * g + 1 - lax.rem(m, 2)
+    hub = 2 * g + 1
 
     def remote(src, dst, send_sem, recv_sem, s, o):
         pltpu.make_async_remote_copy(
@@ -163,7 +164,7 @@
 
         @pl.when(s == sec)
         def _():
-            got(like.at[0 : O - 1], send_sem)
+            got(like.at[:, 0 : O - 1], send_sem)
 
     loads = [
         (order_hbm, order_s),
@@ -227,7 +228,7 @@
                 both = dot(xb, ee_v[...], TN)
                 pt[m, lanes, :] = (both[:, 0:TL] * both[:, TL:]).astype(BF16)
 
-        lax.fori_loop(0, NB, lambda b, c: (one(b), c)[1], 0, unroll=4)
+        lax.fori_loop(0, NB, lambda b, c: (one(b), c)[1], 0, unroll=8)
 
     @pl.when(jnp.logical_not(odd))
     def _():
@@ -237,16 +238,20 @@
     pl.semaphore_wait(barrier, S * O - 1)
 
     def send_lists(s):
-        fan(lambda o: lists, bcr.at[sec, ob], bc_send.at[s], bc_recv.at[sec], s)
+        fan(lambda o: lists, bcr.at[sec * O + ob], bc_send, bc_recv.at[sec], s)
 
     lax.fori_loop(0, S, lambda s, c: (send_lists(s), c)[1], 0)
 
     def send_prior(m):
-        @pl.when(sec == 2 * lax.rem(m, G) + 1)
-        def _():
-            fan(lambda o: pcs.at[m], pcr.at[m, ob], p_send.at[m], p_recv.at[m], 0)
-
-    lax.fori_loop(0, K, lambda m, c: (send_prior(m), c)[1], 0)
+        def one(i):
+            o = lax.rem(m + g, G) + G * i
+            remote(pcs.at[m], pcr.at[m, ob], p_send, p_recv.at[m], 0, o)
+
+        each(0, O // G, one)
+
+    @pl.when(odd)
+    def _():
+        lax.fori_loop(0, K, lambda m, c: (send_prior(m), c)[1], 0)
 
     cs[...] = jnp.zeros_like(cs)
 
@@ -353,7 +358,7 @@
         lane = iota((Q, TL), 1)
         out = jnp.where(lane == T + N, total, jnp.where(lane == T + N + 1, count, out))
         ts[m] = out.reshape(O, SL, TL)
-        fan(lambda o: ts.at[m, o], tr.at[sec, m, ob], t_send.at[m], t_recv.at[sec, m], hub_of(m))
+        fan(lambda o: ts.at[m, o], tr.at[sec, m, ob], t_send, t_recv.at[sec, m], hub)
 
     def scale_of(terms):
         row = iota((Q, TL), 0)
@@ -369,11 +374,16 @@
             cols.append([work[at + 8 * h : at + 8 * h + 8, :] for h in range(H)])
         right = [work[T + 8 * h : T + 8 * h + 8, :] for h in range(H)]
         scale = [jnp.ones((8, Q), F32) for _ in range(H)]
+        pivot_now = jnp.broadcast_to(cols[0][0][0:1], (8, Q))
         for j in range(N):
             h, r = j // 8, j % 8
             col = cols[j]
-            root = lax.rsqrt(jnp.broadcast_to(col[h][r : r + 1], (8, Q)))
+            root = lax.rsqrt(pivot_now)
             inverse = root * root
+            if j + 1 < N:
+                kh, kr = (j + 1) // 8, (j + 1) % 8
+                side = jnp.broadcast_to(col[kh][kr : kr + 1], (8, Q))
+                pivot_now = jnp.broadcast_to(cols[j + 1][kh][kr : kr + 1], (8, Q)) - side * side * inverse
             factor = [v * inverse for v in col]
             factor[h] = jnp.where(sub == r, 0.0, factor[h])
             scale[h] = jnp.where(sub == r, inverse, scale[h])
@@ -388,30 +398,44 @@
                 cols[k][h] = jnp.where(sub == r, pivot, cols[k][h])
         return jnp.concatenate([right[i] * scale[i] for i in range(H)], axis=0)
 
-    def hub_ready(par, m):
-        w = 2 * g + par
-
-        @pl.when(w + 1 < S)
-        def _():
-            base[m] = sum(dot(hots[w + 1, m], part, NT) for part in split3(betas[m]))
-
-        held[m] = sum(dot(part, hots[w, m], NT) for part in split3(state[m]))
+    def base_ready(par, m):
+        after = jnp.minimum(2 * g + par + 1, S - 1)
+        base[m] = sum(dot(hots[after, m], part, NT) for part in split3(betas[m]))
+
+    def at_slots(w, m):
+        return sum(dot(part, hots[w, m], NT) for part in split3(state[m]))
+
+    def full_normal(w, m):
+        terms = tr[w, m].reshape(Q, TL)
+        return sum(dot(part, hots[w, m], TN) for part in split3(terms))[0:T] * scale_of(terms)
+
+    def finish(m):
+        got(state_in.at[m], h_recv.at[m, 0])
+        iob[m] = state_in[m] + full_normal(hub, m)
 
     def hub_entry(par, m):
         w = 2 * g + par
-        hot = hots[w, m]
         got(tr.at[w, m], t_recv.at[w, m])
+
+        @pl.when(par == 0)
+        def _():
+            remote(tr.at[w, m], tr.at[w, m], s_send.at[w], f_recv.at[w, m], sec - 1, ob)
+
         for q in range(1, G):
 
             @pl.when(q > g)
             def _():
-                remote(tr.at[w, m], tr.at[w, m], f_send.at[par, m, q], f_recv.at[w, m], 2 * q + core, ob)
+                remote(tr.at[w, m], tr.at[w, m], f_send.at[par, q], f_recv.at[w, m], 2 * q + 1, ob)
+
+        @pl.when(par == 1)
+        def _():
+            got(held.at[1, m], h_recv.at[m, 1])
 
         terms = tr[w, m].reshape(Q, TL)
         parts = split3(terms)
         inverse = scale_of(terms)
         normal = sum(dot(part, match[par, m], TN) for part in parts) * inverse
-        work[0:T, :] = held[m] + normal[0:T]
+        work[0:T, :] = held[par, m] + normal[0:T]
         work[T:TL, :] = normal[T:TL]
         filled = work[0:1, :] > 0.0
         delta = jnp.where((iota((NP, Q), 0) < N) & filled, solve(), 0.0)
@@ -421,30 +445,33 @@
         def _():
             slots = base[m] + sum(dot(follow[par, m], part, NT) for part in deltas)
             cs[par, m, :, :, 0:NP] = slots.reshape(O, SL, NP)
-            fan(lambda o: cs.at[par, m, o], cr.at[m, ob], c_send.at[par, m], c_recv.at[m], w + 1)
-
-        here = jnp.where(w == sec, 1, 0)
+            fan(lambda o: cs.at[par, m, o], cr.at[m, ob], c_send.at[par], c_recv.at[m], w + 1)
+
         fresh = betas[m] + sum(dot(part, first[par, m], NN) for part in deltas)
         betas[m] = fresh
-        cob[here, m] = fresh
-        post = state[m] + sum(dot(part, hot, TN) for part in parts)[0:T] * inverse
-        iob[here, m] = post
-        state[m] = post * mf_v[...]
-
-        @pl.when(w != sec)
-        def _():
-            remote(iob.at[0, m], iob.at[1, m], o_send.at[m, 0], o_recv.at[m, 0], w, ob)
-            remote(cob.at[0, m], cob.at[1, m], o_send.at[m, 1], o_recv.at[m, 1], w, ob)
-
-        @pl.when((par == 1) & (g + 1 < G))
-        def _():
-            beta_pass[m] = fresh
-            remote(beta_pass.at[m], beta_in.at[m], b_send.at[m], b_recv.at[m], sec + 2, ob)
-
-    def stream(i):
-        return 2 * i + 1 - core
-
-    def hub_begin():
+
+        @pl.when(par == 0)
+        def _():
+            beta_mid[m] = fresh
+            remote(beta_mid.at[m], cob.at[m], o_send, o_recv.at[m], sec - 1, ob)
+            base_ready(1, m)
+
+        @pl.when(par == 1)
+        def _():
+            cob[m] = fresh
+
+            @pl.when(g + 1 < G)
+            def _():
+                remote(cob.at[m], beta_in.at[m], b_send, b_recv.at[m], sec + 2, ob)
+
+            @pl.when(g + 1 == G)
+            def _():
+                finish(m)
+
+    def streams(body):
+        lax.fori_loop(0, K, lambda m, c: (body(m), c)[1], 0)
+
+    def begin():
         pi_in.wait()
         mf_in.wait()
         for m in range(K):
@@ -453,117 +480,140 @@
         prefix = jnp.where(iota((128, 128), 0) <= iota((128, 128), 1), 1.0, 0.0).astype(BF16)
         rank_of_row = (iota((Q, 128), 0) % SL + 1).astype(F32)
         lane = iota((Q, C), 1).astype(F32)
-
         for w in range(S):
-            got(bcr.at[w], bc_recv.at[w])
+            got(bcr.at[w * O : (w + 1) * O], bc_recv.at[w])
         owner_lane = iota((Q, 128), 1) // NB
 
         def window_hots(w):
-            channel = jnp.concatenate([jnp.broadcast_to(bcr[w, o], (SL, 128)) for o in range(O)], axis=0)
+            channel = jnp.concatenate([jnp.broadcast_to(bcr[w * O + o], (SL, 128)) for o in range(O)], axis=0)
             inside = (channel >= low) & (channel < low + C)
-            for i in range(mine):
-                ours = inside & (owner_lane == stream(i))
+            for m in range(K):
+                ours = inside & (owner_lane == m)
                 rank = dot(jnp.where(ours, 1.0, 0.0).astype(BF16), prefix, NN)
                 hit = ours & (rank == rank_of_row)
                 value = jnp.sum(jnp.where(hit, (channel - low + 1).astype(F32), 0.0), axis=1, keepdims=True)
-                hots[w, stream(i)] = jnp.where(lane == value - 1.0, 1.0, 0.0).astype(BF16)
+                hots[w, m] = jnp.where(lane == value - 1.0, 1.0, 0.0).astype(BF16)
 
         each(0, S, window_hots)
+
+    def links():
         earlier_slot = iota((Q, Q), 1) < iota((Q, Q), 0)
-
-        def links(par, i):
-            m = stream(i)
-            w = 2 * g + par
-            hot = hots[w, m]
-            same = dot(hot, hot, NT)
-            match[par, m] = same.astype(BF16)
-            copies = jnp.sum(jnp.where(earlier_slot, same, 0.0), axis=1, keepdims=True)
-            lead = jnp.where(copies == 0.0, hot.astype(F32), 0.0).astype(BF16)
-            first[par, m] = lead
-
-            after = jnp.minimum(w + 1, S - 1)
-            follow[par, m] = dot(hots[after, m], lead, NT).astype(BF16)
-
-        for i in range(mine):
+        for m in range(K):
             for par in range(2):
-                links(par, i)
-
-        def earlier(w):
-            def one(i):
-                m = stream(i)
-                got(tr.at[w, m], f_recv.at[w, m])
-                terms = tr[w, m].reshape(Q, TL)
-                normal = sum(dot(part, hots[w, m], TN) for part in split3(terms))[0:T] * scale_of(terms)
-                state[m] = (state[m] + normal) * mf_v[...]
-
-            lax.fori_loop(0, mine, lambda i, c: (one(i), c)[1], 0)
-
-        lax.fori_loop(0, 2 * g, lambda w, c: (earlier(w), c)[1], 0)
+                w = 2 * g + par
+                hot = hots[w, m]
+                same = dot(hot, hot, NT)
+                match[par, m] = same.astype(BF16)
+                copies = jnp.sum(jnp.where(earlier_slot, same, 0.0), axis=1, keepdims=True)
+                lead = jnp.where(copies == 0.0, hot.astype(F32), 0.0).astype(BF16)
+                first[par, m] = lead
+                after = jnp.minimum(w + 1, S - 1)
+                follow[par, m] = dot(hots[after, m], lead, NT).astype(BF16)
+
+    def catch_up():
+        def one(w, m):
+            got(tr.at[w, m], f_recv.at[w, m])
+
+            @pl.when(odd)
+            def _():
+                remote(tr.at[w, m], tr.at[w, m], s_send.at[w], f_recv.at[w, m], sec - 1, ob)
+
+            state[m] = (state[m] + full_normal(w, m)) * mf_v[...]
+
+        lax.fori_loop(0, 2 * g, lambda w, c: (streams(lambda m: one(w, m)), c)[1], 0)
+
+    def first_ready():
+        def take(m):
+            got(beta_in.at[m], b_recv.at[m])
+            betas[m] = beta_in[m]
 
         @pl.when(g > 0)
         def _():
-            def take(i):
-                m = stream(i)
-                got(beta_in.at[m], b_recv.at[m])
-                betas[m] = beta_in[m]
-
-            lax.fori_loop(0, mine, lambda i, c: (take(i), c)[1], 0)
+            streams(take)
+
+        def one(m):
+            base_ready(0, m)
+            held[0, m] = at_slots(2 * g, m)
+
+        streams(one)
+
+    @pl.when(odd | (g > 0))
+    def _():
+        begin()
+
+    @pl.when(odd)
+    def _():
+        links()
+        catch_up()
+        first_ready()
 
     def turn(par):
         @pl.when(par == core)
         def _():
-            lax.fori_loop(0, K, lambda m, c: (row_entry(m), c)[1], 0)
-
-        @pl.when(par == 0)
-        def _():
-            hub_begin()
-
-        lax.fori_loop(0, mine, lambda i, c: (hub_ready(par, stream(i)), c)[1], 0)
-        lax.fori_loop(0, mine, lambda i, c: (hub_entry(par, stream(i)), c)[1], 0)
+            streams(row_entry)
+
+        @pl.when(odd)
+        def _():
+            streams(lambda m: hub_entry(par, m))
 
     lax.fori_loop(0, 2, lambda par, c: (turn(par), c)[1], 0)
 
-    def arrive(i):
-        m = 2 * i + core
-        got(iob.at[1, m], o_recv.at[m, 0])
-        got(cob.at[1, m], o_recv.at[m, 1])
-
-    lax.fori_loop(0, K - mine, lambda i, c: (arrive(i), c)[1], 0)
+    @pl.when(odd & (g + 1 < G))
+    def _():
+        streams(finish)
+
+    @pl.when(jnp.logical_not(odd))
+    def _():
+        @pl.when(g == 0)
+        def _():
+            begin()
+
+        catch_up()
+
+        def update(m):
+            got(tr.at[2 * g, m], f_recv.at[2 * g, m])
+            post = state[m] + full_normal(2 * g, m)
+            iob[m] = post
+            state[m] = post * mf_v[...]
+            remote(state.at[m], state_in.at[m], h_send.at[0], h_recv.at[m, 0], sec + 1, ob)
+            held[1, m] = at_slots(2 * g + 1, m)
+            remote(held.at[1, m], held.at[1, m], h_send.at[1], h_recv.at[m, 1], sec + 1, ob)
+
+        streams(update)
+        streams(lambda m: got(cob.at[m], o_recv.at[m]))
+
     order_in.wait()
     for k in range(K):
         m = order_s[k]
-        io_out[:, k, :] = iob[1, m]
-        co_out[:, k, :] = cob[1, m, 0:N, :]
-
-    def drain(m):
-        @pl.when(sec == 2 * lax.rem(m, G) + 1)
-        def _():
-            got(pcr.at[m], p_send.at[m])
-
-        fanned(ts.at[m], t_send.at[m], hub_of(m))
-
-    def drain_hub(i):
-        m = stream(i)
-        fanned(cr.at[m], c_send.at[0, m], 2 * g + 1)
+        io_out[:, k, :] = iob[m]
+        co_out[:, k, :] = cob[m, 0:N, :]
+
+    got(bcr.at[0 : S * O - 1], bc_send)
+    fanned(ts, t_send, hub)
+
+    @pl.when(odd)
+    def _():
+        got(pcr.at[:, 0 : O // G], p_send)
+        fanned(cr, c_send.at[0], hub)
+        got(beta_mid, o_send)
+        lax.fori_loop(0, 2 * g + 1, lambda w, c: (got(tr.at[0], s_send.at[w]), c)[1], 0)
 
         @pl.when(g + 1 < G)
         def _():
-            fanned(cr.at[m], c_send.at[1, m], 2 * g + 2)
-            got(betas.at[m], b_send.at[m])
-
-        for par in range(2):
-            for q in range(1, G):
-
-                @pl.when(q > g)
-                def _():
-                    got(ts.at[m], f_send.at[par, m, q])
-
-        got(iob.at[0, m], o_send.at[m, 0])
-        got(cob.at[0, m], o_send.at[m, 1])
-
-    lax.fori_loop(0, mine, lambda i, c: (drain_hub(i), c)[1], 0)
-    lax.fori_loop(0, K, lambda m, c: (drain(m), c)[1], 0)
-    lax.fori_loop(0, S, lambda s, c: (fanned(bcr.at[0], bc_send.at[s], s), c)[1], 0)
+            fanned(cr, c_send.at[1], hub + 1)
+            got(cob, b_send)
+
+        for q in range(1, G):
+
+            @pl.when(q > g)
+            def _():
+                got(tr.at[0], f_send.at[0, q])
+                got(tr.at[0], f_send.at[1, q])
+
+    @pl.when(jnp.logical_not(odd))
+    def _():
+        got(state, h_send.at[0])
+        got(held.at[1], h_send.at[1])
 
 
 def local(
@@ -583,7 +633,7 @@
     NB = block_channel.shape[2]
     R = predictors.shape[3]
     width = R // NB
-    assert width == 128 and S % 2 == 0 and K % 2 == 0 and K * NB <= 128 and NB % 8 == 0
+    assert width == 128 and S % 2 == 0 and O % (S // 2) == 0 and K * NB <= 128 and NB % 8 == 0
     NP = round_up(N + 1, 8)
     SL = round_up(max(2 * NB // O, 1), 8)
     TL = round_up(T + NP + 2, 128)
@@ -624,7 +674,7 @@
             pltpu.VMEM((1, C), F32),
             pltpu.VMEM((NP, 2 * TL), BF16),
             pltpu.VMEM((1, 128), jnp.int32),
-            pltpu.VMEM((S, O, 1, 128), jnp.int32),
+            pltpu.VMEM((S * O, 1, 128), jnp.int32),
             pltpu.VMEM((K, NP, C), F32),
             pltpu.VMEM((K, O, NP, C), F32),
             pltpu.VMEM((2, K, O, SL, 128), F32),
@@ -643,29 +693,33 @@
             pltpu.VMEM((K, NP, C), F32),
             pltpu.VMEM((K, NP, C), F32),
             pltpu.VMEM((K, NP, C), F32),
+            pltpu.VMEM((K, T, C), F32),
             pltpu.VMEM((K, Q, NP), F32),
-            pltpu.VMEM((K, T, Q), F32),
+            pltpu.VMEM((2, K, T, Q), F32),
             pltpu.VMEM((2, K, Q, Q), BF16),
             pltpu.VMEM((2, K, Q, C), BF16),
             pltpu.VMEM((2, K, Q, Q), BF16),
             pltpu.VMEM((TL, Q), F32),
-            pltpu.VMEM((2, K, NP, C), F32),
-            pltpu.VMEM((2, K, T, C), F32),
+            pltpu.VMEM((K, NP, C), F32),
+            pltpu.VMEM((K, T, C), F32),
             dma((10,)),
+            dma,
             dma((S,)),
+            dma,
+            dma((K,)),
+            dma((2,)),
+            dma((K,)),
+            dma,
+            dma((S, K)),
+            dma((2, G)),
+            dma((S, K)),
+            dma,
+            dma((K,)),
             dma((S,)),
+            dma((2,)),
+            dma((K, 2)),
+            dma,
             dma((K,)),
-            dma((K,)),
-            dma((2, K)),
-            dma((K,)),
-            dma((K,)),
-            dma((S, K)),
-            dma((2, K, G)),
-            dma((S, K)),
-            dma((K,)),
-            dma((K,)),
-            dma((K, 2)),
-            dma((K, 2)),
         ],
         compiler_params=pltpu.CompilerParams(
             has_side_effects=True, collective_id=0, vmem_limit_bytes=48 * 1024 * 1024

time: 55.5 us -> 50.2 us (0.905)
  Pallas kernels: 53.2 us -> 47.9 us
    pallas_call x1, Pallas kernels: 53.2 us -> 47.9 us  [local(): pl.pallas_call(functools.partial(kernel, cfg), out_shape=(jax.ShapeDtypeS...]
where the time goes in v3:
time: 50.2 us; the launch traced here: 50.1 us
  Pallas kernels  47.9 us (95%)
  local copies, waits for them, and re-layouts  1.54 us (3%)
  between operations  0.64 us (1%)
    pallas_call x1, Pallas kernels, local(): pl.pallas_call(functools.partial(kernel, cfg), out_shape=(jax.ShapeDtypeS...  47.9 us
    unnamed x2, local copies, waits for them, and re-layouts  1.54 us

profile of v3, /device:TPU:3, one launch (start us, length us, event | category | flops | bytes accessed | tf_op | source)
XLA Modules:
  0.0 50.1 jit_solution(14730149296943089265)
XLA Ops:
  0.6 47.9 %shard_map.113 = (f32[20,4,256]{2,1,0:T(4,128)S(1)}, f32[210,4,256]{2,1,0:T(4,128)S(1)}) custom-call(s32[4]{0:T(128)} %order_hbm.1, bf16[20,4,4096]{2,1,0:T(4,128)(2,1)} %bitcast.31, f32[128,128]{1,0:T(8,128)} %bitcast.33, f32[128,128]{1,0:T(8,128)} %bitcast.34, s32[128,128]{1,0:T(8,128)} %bitcast.35, s32[4,32]{1,0:T(4,128)} %bitcast.36, ...), custom_call_target="tpu_custom_call" | custom-call | tf_op jit(solution)/shard_map/pallas_call | solution.py:657
  48.5 0.6 %copy.17 = f32[1,4,20,256]{3,1,2,0:T(4,128)} copy(f32[1,4,20,256]{3,1,2,0:T(4,128)S(1)} %bitcast.29) | data formatting | bytes 163840
  49.2 0.9 %copy.18 = f32[1,4,210,256]{3,1,2,0:T(4,128)} copy(f32[1,4,210,256]{3,1,2,0:T(4,128)S(1)} %bitcast.28) | data formatting | bytes 1720320

commit v4 on v3

--- a/solution.py
+++ b/solution.py
@@ -83,14 +83,15 @@
     xh,
     pt,
     chcol,
-    place,
-    place_t,
+    slots_v,
+    slots_s,
+    came,
     coef_v,
     hots,
     state,
     betas,
     beta_in,
-    beta_mid,
+    betas_out,
     state_in,
     base,
     held,
@@ -101,6 +102,7 @@
     cob,
     iob,
     load_sem,
+    slot_sem,
     bc_send,
     bc_recv,
     p_send,
@@ -142,12 +144,20 @@
     def got(ref, sem):
         pltpu.make_async_copy(ref, ref, sem).wait()
 
+    def partner(j):
+        if O & (O - 1):
+            return lax.rem(ob + j, O)
+        o = ob
+        for bit in range(O.bit_length() - 1):
+            if j >> bit & 1:
+                step = 1 << bit
+                o = o + step - 2 * step * lax.rem(ob // step, 2)
+        return o
+
     def fan(src, dst, send_sem, recv_sem, s):
-        def one(j):
-            o = lax.rem(ob + j, O)
+        for j in range(1, O):
+            o = partner(O - j)
             remote(src(o), dst, send_sem, recv_sem, s, o)
-
-        each(1, O, one)
 
         @pl.when(s != sec)
         def _():
@@ -164,7 +174,7 @@
 
         @pl.when(s == sec)
         def _():
-            got(like.at[:, 0 : O - 1], send_sem)
+            got(like.at[:, 0 : like.shape[1] // O * (O - 1)], send_sem)
 
     loads = [
         (order_hbm, order_s),
@@ -224,15 +234,22 @@
             lanes = pl.ds(pl.multiple_of(b * 128, 128), 128)
             for m in range(low, high):
                 xb = xs[b, pl.ds(m, NP, stride=K), :].astype(BF16)
-                xh[m, :, lanes] = xb
+                xh[m, b] = xb
                 both = dot(xb, ee_v[...], TN)
-                pt[m, lanes, :] = (both[:, 0:TL] * both[:, TL:]).astype(BF16)
+                product = (both[:, 0:TL] * both[:, TL:]).astype(BF16)
+                for h in range(TL // 128):
+                    pt[m, h, lanes, :] = product[:, 128 * h : 128 * h + 128]
 
         lax.fori_loop(0, NB, lambda b, c: (one(b), c)[1], 0, unroll=8)
 
+    unpack()
+
+    @pl.when(odd)
+    def _():
+        products(0, 1)
+
     @pl.when(jnp.logical_not(odd))
     def _():
-        unpack()
         products(0, K // 2)
 
     pl.semaphore_wait(barrier, S * O - 1)
@@ -254,6 +271,8 @@
         lax.fori_loop(0, K, lambda m, c: (send_prior(m), c)[1], 0)
 
     cs[...] = jnp.zeros_like(cs)
+    coef_v[...] = jnp.zeros_like(coef_v)
+    came[...] = jnp.zeros_like(came)
 
     eye = iota((128, 128), 0) == iota((128, 128), 1)
     upto = iota((128, 128), 0) <= iota((128, 128), 1)
@@ -267,26 +286,23 @@
         range_col = jnp.floor((col + 0.5) * (1.0 / C))
         same = range_row == range_col
         rank_row = jnp.sum(jnp.where(same & upto, 1.0, 0.0), axis=0, keepdims=True)
-        back = jnp.where(same & (iota((128, 128), 0) >= iota((128, 128), 1)), 1.0, 0.0)
-        rank_col = jnp.sum(back, axis=1, keepdims=True)
         chcol[m] = jnp.broadcast_to(col[0:NB], (NB, 128))
-        slot = iota((Q, 128), 0)
-        hit = (range_row[0:1] == (slot // SL).astype(F32)) & (rank_row == (slot % SL + 1).astype(F32))
-        place[m] = jnp.where(hit, 1.0, 0.0).astype(BF16)
-        slot = iota((NB, Q), 1)
-        hit = (range_col[0:NB] == (slot // SL).astype(F32)) & (rank_col[0:NB] == (slot % SL + 1).astype(F32))
-        place_t[m] = jnp.where(hit, 1.0, 0.0).astype(BF16)
+        slots_v[m : m + 1, :] = jnp.clip((range_row[0:1] * float(SL) + rank_row - 1.0).astype(jnp.int32), 0, Q - 1)
+    to_scalars = pltpu.make_async_copy(slots_v, slots_s, slot_sem)
+    to_scalars.start()
 
     @pl.when(odd)
     def _():
-        unpack()
-        products(0, K // 2)
-
-    products(K // 2, K)
+        products(1, K)
+
+    @pl.when(jnp.logical_not(odd))
+    def _():
+        products(K // 2, K)
 
     dep_in.wait()
     prec_in.wait()
     qc_in.wait()
+    to_scalars.wait()
 
     def split_f32(x):
         return [p.astype(F32) for p in split3(x)]
@@ -296,20 +312,26 @@
         def _():
             got(pcr.at[m], p_recv.at[m])
             channel = chcol[m]
-            coef = jnp.zeros((NB, NP), F32)
+            coef = jnp.zeros((NB, N), F32)
             lane = iota((NB, C), 1).astype(F32)
             for o in range(O):
                 wide = jnp.broadcast_to(channel[:, 0:1], (NB, C)) - float(o * C)
                 hot = jnp.where(lane == wide, 1.0, 0.0).astype(BF16)
-                for part in split3(pcr[m, o]):
+                for part in split3(pcr[m, o, 0:N, :]):
                     coef = coef + dot(hot, part, NT)
-            coef_v[...] = coef
+            coef_v[:, 0:N] = coef
 
         @pl.when(sec != 0)
         def _():
             got(cr.at[m], c_recv.at[m])
-            slots = cr[m].reshape(Q, 128)[:, 0:NP]
-            coef_v[...] = sum(dot(place_t[m], part, NN) for part in split3(slots))
+            came[0:Q, :] = cr[m]
+            sub = iota((8, 128), 0)
+            for q in range(NB // 8):
+                tile = jnp.zeros((8, 128), F32)
+                for r in range(8):
+                    row = jnp.broadcast_to(came[pl.ds(jnp.clip(slots_s[m, 8 * q + r], 0, Q - 1), 1), :], (8, 128))
+                    tile = jnp.where(sub == r, row, tile)
+                coef_v[8 * q : 8 * q + 8, :] = tile[:, 0:NP]
 
         pieces = split_f32(coef_v[...])
         sub = iota((8, 128), 0)
@@ -319,7 +341,8 @@
             tile = jnp.zeros((8, 128), F32)
             for c in range(4):
                 at = (8 * q + 2 * c) * 128
-                full = dot(stack, xh[m, :, at : at + 256], NN)
+                pair = jnp.concatenate([xh[m, at // 128], xh[m, at // 128 + 1]], axis=1)
+                full = dot(stack, pair, NN)
                 full = full[0:8] + full[8:16] + full[16:24]
                 tile = jnp.where(sub == 2 * c, full[:, 0:128], tile)
                 tile = jnp.where(sub == 2 * c + 1, full[:, 128:256], tile)
@@ -333,28 +356,21 @@
         pull = weight * residual
         total = jnp.sum(jnp.sum(pull * residual, axis=0, keepdims=True), axis=1, keepdims=True)
         count = jnp.sum(jnp.sum(passed, axis=0, keepdims=True), axis=1, keepdims=True)
-        weight_hi = weight.astype(BF16).astype(F32)
-        weight_lo = weight - weight_hi
-        pull_hi = pull.astype(BF16).astype(F32)
-        pull_lo = pull - pull_hi
-        group = iota((32, 128), 0) % 8
-        lane = iota((8, TL), 1)
-        sums = []
-        for q in range(NB // 8):
-            stack = jnp.concatenate(
-                [v[8 * q : 8 * q + 8] for v in (weight_hi, weight_lo, pull_hi, pull_lo)], axis=0
-            )
-            acc = jnp.zeros((32, TL), F32)
-            for c in range(4):
-                at = (8 * q + 2 * c) * 128
-                left = jnp.concatenate(
-                    [jnp.where(group == 2 * c, stack, 0.0), jnp.where(group == 2 * c + 1, stack, 0.0)], axis=1
+        slot = iota((Q, 128), 0)
+        acc = jnp.zeros((2 * Q, TL), F32)
+        for c in range(NB // 2):
+            sides = []
+            for b in (2 * c, 2 * c + 1):
+                hit = slot == slots_s[m, b]
+                sides.append(
+                    jnp.concatenate(
+                        [jnp.where(hit, jnp.broadcast_to(v[b : b + 1], (Q, 128)), 0.0) for v in (weight, pull)], axis=0
+                    )
                 )
-                acc = acc + dot(left.astype(BF16), pt[m, at : at + 256, :], NN)
-            sums.append(jnp.where(lane < T, acc[0:8] + acc[8:16], acc[16:24] + acc[24:32]))
-        packed = jnp.concatenate(sums, axis=0)
-        place_m = place[m][:, 0:NB]
-        out = sum(dot(place_m, part, NN) for part in split3(packed))
+            left = jnp.concatenate(sides, axis=1).astype(BF16)
+            right = jnp.concatenate([pt[m, h, 256 * c : 256 * c + 256, :] for h in range(TL // 128)], axis=1)
+            acc = acc + dot(left, right, NN)
+        out = jnp.where(iota((Q, TL), 1) < T, acc[0:Q], acc[Q:])
         lane = iota((Q, TL), 1)
         out = jnp.where(lane == T + N, total, jnp.where(lane == T + N + 1, count, out))
         ts[m] = out.reshape(O, SL, TL)
@@ -398,9 +414,10 @@
                 cols[k][h] = jnp.where(sub == r, pivot, cols[k][h])
         return jnp.concatenate([right[i] * scale[i] for i in range(H)], axis=0)
 
-    def base_ready(par, m):
-        after = jnp.minimum(2 * g + par + 1, S - 1)
-        base[m] = sum(dot(hots[after, m], part, NT) for part in split3(betas[m]))
+    def base_ready(m):
+        for par in range(2):
+            after = jnp.minimum(2 * g + par + 1, S - 1)
+            base[par, m] = sum(dot(hots[after, m], part, NT) for part in split3(betas[m]))
 
     def at_slots(w, m):
         return sum(dot(part, hots[w, m], NT) for part in split3(state[m]))
@@ -413,6 +430,15 @@
         got(state_in.at[m], h_recv.at[m, 0])
         iob[m] = state_in[m] + full_normal(hub, m)
 
+    def change(par, m):
+        w = 2 * g + par
+        terms = tr[w, m].reshape(Q, TL)
+        normal = sum(dot(part, match[par, m], TN) for part in split3(terms)) * scale_of(terms)
+        work[0:T, :] = held[par, m] + normal[0:T]
+        work[T:TL, :] = normal[T:TL]
+        filled = work[0:1, :] > 0.0
+        return split3(jnp.where((iota((NP, Q), 0) < N) & filled, solve(), 0.0))
+
     def hub_entry(par, m):
         w = 2 * g + par
         got(tr.at[w, m], t_recv.at[w, m])
@@ -431,42 +457,32 @@
         def _():
             got(held.at[1, m], h_recv.at[m, 1])
 
-        terms = tr[w, m].reshape(Q, TL)
-        parts = split3(terms)
-        inverse = scale_of(terms)
-        normal = sum(dot(part, match[par, m], TN) for part in parts) * inverse
-        work[0:T, :] = held[par, m] + normal[0:T]
-        work[T:TL, :] = normal[T:TL]
-        filled = work[0:1, :] > 0.0
-        delta = jnp.where((iota((NP, Q), 0) < N) & filled, solve(), 0.0)
-        deltas = split3(delta)
-
         @pl.when(w + 1 < S)
         def _():
-            slots = base[m] + sum(dot(follow[par, m], part, NT) for part in deltas)
+            deltas = change(par, m)
+            slots = base[par, m] + sum(dot(follow[par, m], part, NT) for part in deltas)
+            later = base[1, m] + sum(dot(follow[2, m], part, NT) for part in deltas)
+            fresh = betas[m] + sum(dot(part, first[par, m], NN) for part in deltas)
             cs[par, m, :, :, 0:NP] = slots.reshape(O, SL, NP)
-            fan(lambda o: cs.at[par, m, o], cr.at[m, ob], c_send.at[par], c_recv.at[m], w + 1)
-
-        fresh = betas[m] + sum(dot(part, first[par, m], NN) for part in deltas)
-        betas[m] = fresh
-
-        @pl.when(par == 0)
-        def _():
-            beta_mid[m] = fresh
-            remote(beta_mid.at[m], cob.at[m], o_send, o_recv.at[m], sec - 1, ob)
-            base_ready(1, m)
-
-        @pl.when(par == 1)
-        def _():
-            cob[m] = fresh
-
-            @pl.when(g + 1 < G)
+            base[1, m] = later
+            betas[m] = fresh
+            betas_out[par, m] = fresh
+            fan(lambda o: cs.at[par, m, o], cr.at[m, pl.ds(pl.multiple_of(ob * SL, SL), SL)], c_send.at[par], c_recv.at[m], w + 1)
+
+            @pl.when(par == 0)
             def _():
-                remote(cob.at[m], beta_in.at[m], b_send, b_recv.at[m], sec + 2, ob)
-
-            @pl.when(g + 1 == G)
+                remote(betas_out.at[0, m], cob.at[m], o_send, o_recv.at[m], sec - 1, ob)
+
+            @pl.when(par == 1)
             def _():
-                finish(m)
+                cob[m] = betas_out[1, m]
+                remote(betas_out.at[1, m], beta_in.at[m], b_send, b_recv.at[m], sec + 2, ob)
+
+        @pl.when(w + 1 == S)
+        def _():
+            got(state_in.at[m], h_recv.at[m, 0])
+            iob[m] = state_in[m] + full_normal(hub, m)
+            cob[m] = betas[m] + sum(dot(part, first[par, m], NN) for part in change(par, m))
 
     def streams(body):
         lax.fori_loop(0, K, lambda m, c: (body(m), c)[1], 0)
@@ -500,42 +516,53 @@
         earlier_slot = iota((Q, Q), 1) < iota((Q, Q), 0)
         for m in range(K):
             for par in range(2):
-                w = 2 * g + par
-                hot = hots[w, m]
+                hot = hots[2 * g + par, m]
                 same = dot(hot, hot, NT)
                 match[par, m] = same.astype(BF16)
                 copies = jnp.sum(jnp.where(earlier_slot, same, 0.0), axis=1, keepdims=True)
-                lead = jnp.where(copies == 0.0, hot.astype(F32), 0.0).astype(BF16)
-                first[par, m] = lead
-                after = jnp.minimum(w + 1, S - 1)
-                follow[par, m] = dot(hots[after, m], lead, NT).astype(BF16)
-
-    def catch_up():
-        def one(w, m):
-            got(tr.at[w, m], f_recv.at[w, m])
-
-            @pl.when(odd)
+                first[par, m] = jnp.where(copies == 0.0, hot.astype(F32), 0.0).astype(BF16)
+        after = jnp.minimum(2 * g + 2, S - 1)
+        for m in range(K):
+            follow[0, m] = dot(hots[2 * g + 1, m], first[0, m], NT).astype(BF16)
+            follow[1, m] = dot(hots[after, m], first[1, m], NT).astype(BF16)
+            follow[2, m] = dot(hots[after, m], first[0, m], NT).astype(BF16)
+
+    def catch_up_one(w, m):
+        got(tr.at[w, m], f_recv.at[w, m])
+
+        @pl.when(odd)
+        def _():
+            remote(tr.at[w, m], tr.at[w, m], s_send.at[w], f_recv.at[w, m], sec - 1, ob)
+
+        state[m] = (state[m] + full_normal(w, m)) * mf_v[...]
+
+    def catch_up(windows):
+        lax.fori_loop(0, windows, lambda w, c: (streams(lambda m: catch_up_one(w, m)), c)[1], 0)
+
+    def first_ready():
+        @pl.when(g == 0)
+        def _():
+            for m in range(K):
+                base_ready(m)
+                held[0, m] = at_slots(2 * g, m)
+
+        def one(i):
+            @pl.when(i < K)
             def _():
-                remote(tr.at[w, m], tr.at[w, m], s_send.at[w], f_recv.at[w, m], sec - 1, ob)
-
-            state[m] = (state[m] + full_normal(w, m)) * mf_v[...]
-
-        lax.fori_loop(0, 2 * g, lambda w, c: (streams(lambda m: one(w, m)), c)[1], 0)
-
-    def first_ready():
-        def take(m):
-            got(beta_in.at[m], b_recv.at[m])
-            betas[m] = beta_in[m]
+                m = jnp.minimum(i, K - 1)
+                catch_up_one(2 * g - 1, m)
+                held[0, m] = at_slots(2 * g, m)
+
+            @pl.when(i >= 2)
+            def _():
+                m = jnp.maximum(i - 2, 0)
+                got(beta_in.at[m], b_recv.at[m])
+                betas[m] = beta_in[m]
+                base_ready(m)
 
         @pl.when(g > 0)
         def _():
-            streams(take)
-
-        def one(m):
-            base_ready(0, m)
-            held[0, m] = at_slots(2 * g, m)
-
-        streams(one)
+            lax.fori_loop(0, K + 2, lambda i, c: (one(i), c)[1], 0)
 
     @pl.when(odd | (g > 0))
     def _():
@@ -544,8 +571,10 @@
     @pl.when(odd)
     def _():
         links()
-        catch_up()
+        catch_up(2 * g - 1)
         first_ready()
+        got(pcr.at[:, 0 : O // G], p_send)
+        lax.fori_loop(0, 2 * g, lambda w, c: (got(tr.at[0], s_send.at[w]), c)[1], 0)
 
     def turn(par):
         @pl.when(par == core)
@@ -556,6 +585,7 @@
         def _():
             streams(lambda m: hub_entry(par, m))
 
+    got(bcr.at[0 : S * O - 1], bc_send)
     lax.fori_loop(0, 2, lambda par, c: (turn(par), c)[1], 0)
 
     @pl.when(odd & (g + 1 < G))
@@ -568,7 +598,7 @@
         def _():
             begin()
 
-        catch_up()
+        catch_up(2 * g)
 
         def update(m):
             got(tr.at[2 * g, m], f_recv.at[2 * g, m])
@@ -588,20 +618,18 @@
         io_out[:, k, :] = iob[m]
         co_out[:, k, :] = cob[m, 0:N, :]
 
-    got(bcr.at[0 : S * O - 1], bc_send)
     fanned(ts, t_send, hub)
 
     @pl.when(odd)
     def _():
-        got(pcr.at[:, 0 : O // G], p_send)
         fanned(cr, c_send.at[0], hub)
-        got(beta_mid, o_send)
-        lax.fori_loop(0, 2 * g + 1, lambda w, c: (got(tr.at[0], s_send.at[w]), c)[1], 0)
+        got(betas_out.at[0], o_send)
+        got(tr.at[0], s_send.at[2 * g])
 
         @pl.when(g + 1 < G)
         def _():
             fanned(cr, c_send.at[1], hub + 1)
-            got(cob, b_send)
+            got(betas_out.at[1], b_send)
 
         for q in range(1, G):
 
@@ -678,31 +706,33 @@
             pltpu.VMEM((K, NP, C), F32),
             pltpu.VMEM((K, O, NP, C), F32),
             pltpu.VMEM((2, K, O, SL, 128), F32),
-            pltpu.VMEM((K, O, SL, 128), F32),
+            pltpu.VMEM((K, Q, 128), F32),
             pltpu.VMEM((K, O, SL, TL), F32),
             pltpu.VMEM((S, K, O, SL, TL), F32),
             pltpu.VMEM((NB, NP * K, 128), F32),
-            pltpu.VMEM((K, NP, R), BF16),
-            pltpu.VMEM((K, R, TL), BF16),
+            pltpu.VMEM((K, NB, NP, 128), BF16),
+            pltpu.VMEM((K, TL // 128, R, 128), BF16),
             pltpu.VMEM((K, NB, 128), F32),
-            pltpu.VMEM((K, Q, 128), BF16),
-            pltpu.VMEM((K, NB, Q), BF16),
+            pltpu.VMEM((K, 128), jnp.int32),
+            pltpu.SMEM((K, 128), jnp.int32),
+            pltpu.VMEM((Q + 8, 128), F32),
             pltpu.VMEM((NB, NP), F32),
             pltpu.VMEM((S, K, Q, C), BF16),
             pltpu.VMEM((K, T, C), F32),
             pltpu.VMEM((K, NP, C), F32),
             pltpu.VMEM((K, NP, C), F32),
-            pltpu.VMEM((K, NP, C), F32),
+            pltpu.VMEM((2, K, NP, C), F32),
             pltpu.VMEM((K, T, C), F32),
-            pltpu.VMEM((K, Q, NP), F32),
+            pltpu.VMEM((2, K, Q, NP), F32),
             pltpu.VMEM((2, K, T, Q), F32),
             pltpu.VMEM((2, K, Q, Q), BF16),
             pltpu.VMEM((2, K, Q, C), BF16),
-            pltpu.VMEM((2, K, Q, Q), BF16),
+            pltpu.VMEM((3, K, Q, Q), BF16),
             pltpu.VMEM((TL, Q), F32),
             pltpu.VMEM((K, NP, C), F32),
             pltpu.VMEM((K, T, C), F32),
             dma((10,)),
+            dma,
             dma,
             dma((S,)),
             dma,

time: 50.2 us -> 46.5 us (0.926)
  Pallas kernels: 47.9 us -> 44.2 us
    pallas_call x1, Pallas kernels: 47.9 us -> 44.2 us  [local(): pl.pallas_call(functools.partial(kernel, cfg), out_shape=(jax.ShapeDtypeS...]
where the time goes in v4:
time: 46.5 us; the launch traced here: 46.4 us
  Pallas kernels  44.2 us (95%)
  local copies, waits for them, and re-layouts  1.54 us (3%)
  between operations  0.64 us (1%)
    pallas_call x1, Pallas kernels, local(): pl.pallas_call(functools.partial(kernel, cfg), out_shape=(jax.ShapeDtypeS...  44.2 us
    unnamed x2, local copies, waits for them, and re-layouts  1.54 us

profile of v4, /device:TPU:3, one launch (start us, length us, event | category | flops | bytes accessed | tf_op | source)
XLA Modules:
  0.0 46.4 jit_solution(14406372294798940181)
XLA Ops:
  0.6 44.2 %shard_map.113 = (f32[20,4,256]{2,1,0:T(4,128)S(1)}, f32[210,4,256]{2,1,0:T(4,128)S(1)}) custom-call(s32[4]{0:T(128)} %order_hbm.1, bf16[20,4,4096]{2,1,0:T(4,128)(2,1)} %bitcast.31, f32[128,128]{1,0:T(8,128)} %bitcast.33, f32[128,128]{1,0:T(8,128)} %bitcast.34, s32[128,128]{1,0:T(8,128)} %bitcast.35, s32[4,32]{1,0:T(4,128)} %bitcast.36, ...), custom_call_target="tpu_custom_call" | custom-call | tf_op jit(solution)/shard_map/pallas_call | solution.py:685
  44.8 0.6 %copy.17 = f32[1,4,20,256]{3,1,2,0:T(4,128)} copy(f32[1,4,20,256]{3,1,2,0:T(4,128)S(1)} %bitcast.29) | data formatting | bytes 163840
  45.5 0.9 %copy.18 = f32[1,4,210,256]{3,1,2,0:T(4,128)} copy(f32[1,4,210,256]{3,1,2,0:T(4,128)S(1)} %bitcast.28) | data formatting | bytes 1720320

commit v5 on v4

--- a/solution.py
+++ b/solution.py
@@ -27,6 +27,11 @@
     mid = rest.astype(BF16)
     low = (rest - mid.astype(F32)).astype(BF16)
     return hi, mid, low
+
+
+def split2(x):
+    hi = x.astype(BF16)
+    return hi, (x - hi.astype(F32)).astype(BF16)
 
 
 def dot(a, b, dims):
@@ -257,8 +262,6 @@
     def send_lists(s):
         fan(lambda o: lists, bcr.at[sec * O + ob], bc_send, bc_recv.at[sec], s)
 
-    lax.fori_loop(0, S, lambda s, c: (send_lists(s), c)[1], 0)
-
     def send_prior(m):
         def one(i):
             o = lax.rem(m + g, G) + G * i
@@ -269,6 +272,8 @@
     @pl.when(odd)
     def _():
         lax.fori_loop(0, K, lambda m, c: (send_prior(m), c)[1], 0)
+
+    lax.fori_loop(0, S, lambda s, c: (send_lists(s), c)[1], 0)
 
     cs[...] = jnp.zeros_like(cs)
     coef_v[...] = jnp.zeros_like(coef_v)
@@ -305,7 +310,7 @@
     to_scalars.wait()
 
     def split_f32(x):
-        return [p.astype(F32) for p in split3(x)]
+        return [p.astype(F32) for p in split2(x)]
 
     def row_entry(m):
         @pl.when(sec == 0)
@@ -317,7 +322,7 @@
             for o in range(O):
                 wide = jnp.broadcast_to(channel[:, 0:1], (NB, C)) - float(o * C)
                 hot = jnp.where(lane == wide, 1.0, 0.0).astype(BF16)
-                for part in split3(pcr[m, o, 0:N, :]):
+                for part in split2(pcr[m, o, 0:N, :]):
                     coef = coef + dot(hot, part, NT)
             coef_v[:, 0:N] = coef
 
@@ -343,7 +348,7 @@
                 at = (8 * q + 2 * c) * 128
                 pair = jnp.concatenate([xh[m, at // 128], xh[m, at // 128 + 1]], axis=1)
                 full = dot(stack, pair, NN)
-                full = full[0:8] + full[8:16] + full[16:24]
+                full = full[0:8] + full[8:16]
                 tile = jnp.where(sub == 2 * c, full[:, 0:128], tile)
                 tile = jnp.where(sub == 2 * c + 1, full[:, 128:256], tile)
             tiles.append(tile)
@@ -424,7 +429,7 @@
 
     def full_normal(w, m):
         terms = tr[w, m].reshape(Q, TL)
-        return sum(dot(part, hots[w, m], TN) for part in split3(terms))[0:T] * scale_of(terms)
+        return sum(dot(part, hots[w, m], TN) for part in split2(terms))[0:T] * scale_of(terms)
 
     def finish(m):
         got(state_in.at[m], h_recv.at[m, 0])
@@ -433,11 +438,11 @@
     def change(par, m):
         w = 2 * g + par
         terms = tr[w, m].reshape(Q, TL)
-        normal = sum(dot(part, match[par, m], TN) for part in split3(terms)) * scale_of(terms)
+        normal = sum(dot(part, match[par, m], TN) for part in split2(terms)) * scale_of(terms)
         work[0:T, :] = held[par, m] + normal[0:T]
         work[T:TL, :] = normal[T:TL]
         filled = work[0:1, :] > 0.0
-        return split3(jnp.where((iota((NP, Q), 0) < N) & filled, solve(), 0.0))
+        return split2(jnp.where((iota((NP, Q), 0) < N) & filled, solve(), 0.0))
 
     def hub_entry(par, m):
         w = 2 * g + par
@@ -642,6 +647,17 @@
     def _():
         got(state, h_send.at[0])
         got(held.at[1], h_send.at[1])
+
+
+def write_out(coeffs, info, coeffs_out, info_out, sems):
+    copies = [
+        pltpu.make_async_copy(info, info_out, sems.at[0]),
+        pltpu.make_async_copy(coeffs, coeffs_out, sems.at[1]),
+    ]
+    for copy in copies:
+        copy.start()
+    for copy in copies:
+        copy.wait()
 
 
 def local(
@@ -766,6 +782,17 @@
         memory_factor[None],
         jnp.asarray(expand, BF16),
     )))
+    coeffs, info = pl.pallas_call(
+        write_out,
+        out_shape=(
+            jax.ShapeDtypeStruct((N, K, C), F32),
+            jax.ShapeDtypeStruct((T, K, C), F32),
+        ),
+        in_specs=[vm, vm],
+        out_specs=(hbm, hbm),
+        scratch_shapes=[dma((2,))],
+        compiler_params=pltpu.CompilerParams(vmem_limit_bytes=4 * 1024 * 1024),
+    )(coeffs, info)
     return coeffs.transpose(1, 0, 2)[None], info.transpose(1, 0, 2)[None]
 
 

time: 46.5 us -> 45.5 us (0.978)
  local copies, waits for them, and re-layouts: 1.54 us -> 0 us
  Pallas kernels: 44.2 us -> 44.7 us
    unnamed x2 -> x0, local copies, waits for them, and re-layouts: 1.54 us -> none
    pallas_call x0 -> x1, Pallas kernels: none -> 0.94 us  [local(): pl.pallas_call(write_out, out_shape=(jax.ShapeDtypeStruct((N, K, C), F32)...]
where the time goes in v5:
time: 45.5 us; the launch traced here: 45.3 us
  Pallas kernels  44.7 us (98%)
  between operations  0.64 us (1%)
    pallas_call x1, Pallas kernels, local(): pl.pallas_call(functools.partial(kernel, cfg), out_shape=(jax.ShapeDtypeS...  43.8 us
    pallas_call x1, Pallas kernels, local(): pl.pallas_call(write_out, out_shape=(jax.ShapeDtypeStruct((N, K, C), F32)...  0.94 us

profile of v5, /device:TPU:3, one launch (start us, length us, event | category | flops | bytes accessed | tf_op | source)
XLA Modules:
  0.0 45.3 jit_solution(558743470323019815)
XLA Ops:
  0.6 43.8 %shard_map.113 = (f32[20,4,256]{2,1,0:T(4,128)S(1)}, f32[210,4,256]{2,1,0:T(4,128)S(1)}) custom-call(s32[4]{0:T(128)} %order_hbm.1, bf16[20,4,4096]{2,1,0:T(4,128)(2,1)} %bitcast.29, f32[128,128]{1,0:T(8,128)} %bitcast.31, f32[128,128]{1,0:T(8,128)} %bitcast.32, s32[128,128]{1,0:T(8,128)} %bitcast.33, s32[4,32]{1,0:T(4,128)} %bitcast.34, ...), custom_call_target="tpu_custom_call" | custom-call | tf_op jit(solution)/shard_map/pallas_call | solution.py:701
  44.4 0.9 %shard_map.114 = (f32[20,4,256]{2,1,0:T(4,128)}, f32[210,4,256]{2,1,0:T(4,128)}) custom-call(f32[20,4,256]{2,1,0:T(4,128)S(1)} %get-tuple-element.6.coeffs, f32[210,4,256]{2,1,0:T(4,128)S(1)} %get-tuple-element.7.info), custom_call_target="tpu_custom_call" | custom-call | tf_op jit(solution)/shard_map/pallas_call | solution.py:785

commit v6 on v5

--- a/solution.py
+++ b/solution.py
@@ -149,15 +149,18 @@
     def got(ref, sem):
         pltpu.make_async_copy(ref, ref, sem).wait()
 
-    def partner(j):
-        if O & (O - 1):
-            return lax.rem(ob + j, O)
-        o = ob
-        for bit in range(O.bit_length() - 1):
+    def flipped(at, j, n):
+        if n & (n - 1):
+            return lax.rem(at + j, n)
+        o = at
+        for bit in range(n.bit_length() - 1):
             if j >> bit & 1:
                 step = 1 << bit
-                o = o + step - 2 * step * lax.rem(ob // step, 2)
+                o = o + step - 2 * step * lax.rem(at // step, 2)
         return o
+
+    def partner(j):
+        return flipped(ob, j, O)
 
     def fan(src, dst, send_sem, recv_sem, s):
         for j in range(1, O):
@@ -194,10 +197,6 @@
         (pi_hbm, pi_v),
     ]
     loads = [pltpu.make_async_copy(a, b, load_sem.at[i]) for i, (a, b) in enumerate(loads)]
-    for copy in loads:
-        copy.start()
-    order_in, bc_in, pc_in, x_in, ee_in, dep_in, prec_in, qc_in, mf_in, pi_in = loads
-
     barrier = pltpu.get_barrier_semaphore()
 
     def greet(s):
@@ -214,6 +213,9 @@
         each(0, O, one)
 
     lax.fori_loop(0, S, lambda s, c: (greet(s), c)[1], 0)
+    for copy in loads:
+        copy.start()
+    order_in, bc_in, pc_in, x_in, ee_in, dep_in, prec_in, qc_in, mf_in, pi_in = loads
 
     bc_in.wait()
     line = [bc_v[m : m + 1, :] for m in range(K)]
@@ -263,11 +265,9 @@
         fan(lambda o: lists, bcr.at[sec * O + ob], bc_send, bc_recv.at[sec], s)
 
     def send_prior(m):
-        def one(i):
-            o = lax.rem(m + g, G) + G * i
+        for j in reversed(range(O // G)):
+            o = lax.rem(m + g, G) + G * flipped(ob // G, j, O // G)
             remote(pcs.at[m], pcr.at[m, ob], p_send, p_recv.at[m], 0, o)
-
-        each(0, O // G, one)
 
     @pl.when(odd)
     def _():

time: 45.5 us -> 45.4 us (level)
  no operation moved by 1% of the time
where the time goes in v6:
time: 45.4 us; the launch traced here: 45.2 us
  Pallas kernels  44.6 us (98%)
  between operations  0.64 us (1%)
    pallas_call x1, Pallas kernels, local(): pl.pallas_call(functools.partial(kernel, cfg), out_shape=(jax.ShapeDtypeS...  43.6 us
    pallas_call x1, Pallas kernels, local(): pl.pallas_call(write_out, out_shape=(jax.ShapeDtypeStruct((N, K, C), F32)...  0.94 us

profile of v6, /device:TPU:3, one launch (start us, length us, event | category | flops | bytes accessed | tf_op | source)
XLA Modules:
  0.0 45.2 jit_solution(16111487701187597227)
XLA Ops:
  0.6 43.6 %shard_map.113 = (f32[20,4,256]{2,1,0:T(4,128)S(1)}, f32[210,4,256]{2,1,0:T(4,128)S(1)}) custom-call(s32[4]{0:T(128)} %order_hbm.1, bf16[20,4,4096]{2,1,0:T(4,128)(2,1)} %bitcast.29, f32[128,128]{1,0:T(8,128)} %bitcast.31, f32[128,128]{1,0:T(8,128)} %bitcast.32, s32[128,128]{1,0:T(8,128)} %bitcast.33, s32[4,32]{1,0:T(4,128)} %bitcast.34, ...), custom_call_target="tpu_custom_call" | custom-call | tf_op jit(solution)/shard_map/pallas_call | solution.py:701
  44.3 0.9 %shard_map.114 = (f32[20,4,256]{2,1,0:T(4,128)}, f32[210,4,256]{2,1,0:T(4,128)}) custom-call(f32[20,4,256]{2,1,0:T(4,128)S(1)} %get-tuple-element.6.coeffs, f32[210,4,256]{2,1,0:T(4,128)S(1)} %get-tuple-element.7.info), custom_call_target="tpu_custom_call" | custom-call | tf_op jit(solution)/shard_map/pallas_call | solution.py:785

commit v7 on v6

--- a/solution.py
+++ b/solution.py
@@ -315,15 +315,14 @@
     def row_entry(m):
         @pl.when(sec == 0)
         def _():
+            wide = jnp.concatenate([chcol[m]] * -(-C // 128), axis=1)[:, 0:C]
+            lane = iota((NB, C), 1).astype(F32)
+            picks = [jnp.where(lane == wide - float(o * C), 1.0, 0.0).astype(BF16) for o in range(O)]
             got(pcr.at[m], p_recv.at[m])
-            channel = chcol[m]
             coef = jnp.zeros((NB, N), F32)
-            lane = iota((NB, C), 1).astype(F32)
             for o in range(O):
-                wide = jnp.broadcast_to(channel[:, 0:1], (NB, C)) - float(o * C)
-                hot = jnp.where(lane == wide, 1.0, 0.0).astype(BF16)
                 for part in split2(pcr[m, o, 0:N, :]):
-                    coef = coef + dot(hot, part, NT)
+                    coef = coef + dot(picks[o], part, NT)
             coef_v[:, 0:N] = coef
 
         @pl.when(sec != 0)

time: 45.4 us -> 45.3 us (level)
  no operation moved by 1% of the time
where the time goes in v7:
time: 45.3 us; the launch traced here: 45.1 us
  Pallas kernels  44.5 us (98%)
  between operations  0.64 us (1%)
    pallas_call x1, Pallas kernels, local(): pl.pallas_call(functools.partial(kernel, cfg), out_shape=(jax.ShapeDtypeS...  43.6 us
    pallas_call x1, Pallas kernels, local(): pl.pallas_call(write_out, out_shape=(jax.ShapeDtypeStruct((N, K, C), F32)...  0.94 us

profile of v7, /device:TPU:3, one launch (start us, length us, event | category | flops | bytes accessed | tf_op | source)
XLA Modules:
  0.0 45.1 jit_solution(13380785498615304380)
XLA Ops:
  0.6 43.6 %shard_map.113 = (f32[20,4,256]{2,1,0:T(4,128)S(1)}, f32[210,4,256]{2,1,0:T(4,128)S(1)}) custom-call(s32[4]{0:T(128)} %order_hbm.1, bf16[20,4,4096]{2,1,0:T(4,128)(2,1)} %bitcast.29, f32[128,128]{1,0:T(8,128)} %bitcast.31, f32[128,128]{1,0:T(8,128)} %bitcast.32, s32[128,128]{1,0:T(8,128)} %bitcast.33, s32[4,32]{1,0:T(4,128)} %bitcast.34, ...), custom_call_target="tpu_custom_call" | custom-call | tf_op jit(solution)/shard_map/pallas_call | solution.py:700
  44.2 0.9 %shard_map.114 = (f32[20,4,256]{2,1,0:T(4,128)}, f32[210,4,256]{2,1,0:T(4,128)}) custom-call(f32[20,4,256]{2,1,0:T(4,128)S(1)} %get-tuple-element.6.coeffs, f32[210,4,256]{2,1,0:T(4,128)S(1)} %get-tuple-element.7.info), custom_call_target="tpu_custom_call" | custom-call | tf_op jit(solution)/shard_map/pallas_call | solution.py:784
